TPU v7x, 256 devices: a whole 4x4x8 slice. The times are simulated.
256 devices in a mesh: tensor: 8 (over z), expert: 2 (over core), dp: 16 (over y, x).
Axes of the slice: x: 4, y: 4, z: 8, core: 2. Of those that a mesh axis runs over, the one named last changes fastest.
Arguments:
- tokens: bfloat16 [4096, 2048], P(('expert', 'dp')), may hold values from -6 to 6
- tangent: bfloat16 [4096, 2048], P(('expert', 'dp')), may hold values from -6 to 6
- cotangent: bfloat16 [4096, 2048], P(('expert', 'dp')), may hold values from -0.59765625 to 0.59765625
- expert_ids: int32 [4096, 8], P(('expert', 'dp')), may hold values from 0 to 15, all different within a row; in each aligned block of 128 rows (0 to 127, 128 to 255, ...) at most 96 rows name the same one
- gates: float32 [4096, 8], P(('expert', 'dp')), may hold values from 0.1 to 1
- w_in: bfloat16 [16, 2, 768, 2048], P(('tensor', 'expert'), None, None, 'dp'), may hold values from -0.125 to 0.125
- v_in: bfloat16 [16, 2, 768, 2048], P(('tensor', 'expert'), None, None, 'dp'), may hold values from -0.125 to 0.125
- w_out: bfloat16 [16, 768, 2048], P(('tensor', 'expert'), None, 'dp'), may hold values from -0.21875 to 0.21875
- v_out: bfloat16 [16, 768, 2048], P(('tensor', 'expert'), None, 'dp'), may hold values from -0.21875 to 0.21875
Outputs:
- hvp_tokens: float32 [4096, 2048], P(('expert', 'dp'))
- hvp_in: float32 [16, 2, 768, 2048], P(('tensor', 'expert'), None, None, 'dp')
- hvp_out: float32 [16, 768, 2048], P(('tensor', 'expert'), None, 'dp')
Inputs may be any that keep to these rules, and one draw needn't show every extreme that they name: `expert_ids`: each token names 8 different experts; among the tokens of one block of 128 no expert is named more than 96 times, and some expert reaches 96 in some blocks.
All inputs are finite; a program needn't handle non-finite values.
Results may differ from a plain program's by a relative error of at most 0.013.
Values may be sent and summed in bfloat16 or wider, within the bound.
A program may use at most 128 MiB of HBM per device.

v0:
```python
import functools

import jax
import jax.numpy as jnp
from jax import lax
from jax.experimental import pallas as pl
from jax.experimental.pallas import tpu as pltpu
from jax.sharding import PartitionSpec as P

MESH = pl.DeviceIdType.MESH
F32 = jnp.float32
BF16 = jnp.bfloat16
SIDE = 4
NT = (((1,), (1,)), ((), ()))
NN = (((1,), (0,)), ((), ()))


def mm(a, b, dims=NN):
    return lax.dot_general(a, b, dims, preferred_element_type=F32)


def kernel(
    n_z, ids_ref, gates_ref, tok_ref, tan_ref, cot_ref, wi_ref, vi_ref, wo_ref, vo_ref,
    out_tok, out_in, out_out,
    W, X, G, C, S, ST, H, acc, Pown, PDs, PDr, xs, xopp, xr, xropp, ys, yopp, yr, yropp, R, OUT, Zs, Zr, Zf,
    loc, wa_s, wa_r, wy_s, wy_r, wf_s, wf_r, xh_s, xh_r, xf_s, xf_r, g_s, g_r, gd, dd_s, dd_r, pd_s, pd_r,
    xo_s, xo_r, xp_s, xp_r, yo_s, yo_r, yp_s, yp_r, ra_s, ra_r, z1_s, z1_r, z2_s, z2_r,
):
    t = lax.axis_index("tensor")
    e = lax.axis_index("expert")
    p = lax.axis_index("dp")
    y, x = p // SIDE, p % SIDE
    tok = tok_ref.shape[0]
    half = tok // 2
    lanes = wi_ref.shape[-1]
    q = W.shape[1]
    width = W.shape[2]
    part = width // SIDE

    def at_x(d):
        return lax.rem(x + d, SIDE)

    def at_y(d):
        return lax.rem(y + d, SIDE)

    def dev_x(d):
        return (t, e, y * SIDE + at_x(d))

    def dev_y(d):
        return (t, e, at_y(d) * SIDE + x)

    def dev_z(d):
        return (lax.rem(t + d, n_z), e, p)

    partner = (t, 1 - e, p)
    pending = []

    def send(src, dst, ssem, rsem, dev):
        copy = pltpu.make_async_remote_copy(
            src_ref=src, dst_ref=dst, send_sem=ssem, recv_sem=rsem, device_id=dev, device_id_type=MESH
        )
        copy.start()
        pending.append(copy)

    def got(dst, ssem, rsem):
        pltpu.make_async_remote_copy(
            src_ref=dst, dst_ref=dst, send_sem=ssem, recv_sem=rsem, device_id=partner, device_id_type=MESH
        ).wait_recv()

    barrier = pltpu.get_barrier_semaphore()
    peers = [partner] + [dev_x(d) for d in (1, 2, 3)] + [dev_y(d) for d in (1, 3)] + [dev_z(d) for d in range(1, n_z)]
    for peer in peers:
        pl.semaphore_signal(barrier, inc=1, device_id=peer, device_id_type=MESH)

    def slab(yy, xx):
        return pl.ds(pl.multiple_of((yy * SIDE + xx) * lanes, lanes), lanes)

    def rows(k):
        return pl.ds(pl.multiple_of(k * q, q), q)

    mine = [
        pltpu.make_async_copy(tok_ref, X.at[0, x, e], loc.at[0]),
        pltpu.make_async_copy(tan_ref, X.at[1, x, e], loc.at[1]),
        pltpu.make_async_copy(cot_ref, X.at[2, x, e], loc.at[2]),
        pltpu.make_async_copy(wi_ref.at[:, rows(x), :], W.at[0:2, :, slab(y, x)], loc.at[3]),
        pltpu.make_async_copy(vi_ref.at[:, rows(x), :], W.at[2:4, :, slab(y, x)], loc.at[4]),
        pltpu.make_async_copy(wo_ref.at[rows(x), :], W.at[4, :, slab(y, x)], loc.at[5]),
        pltpu.make_async_copy(vo_ref.at[rows(x), :], W.at[5, :, slab(y, x)], loc.at[6]),
    ]
    for copy in mine:
        copy.start()
    ids, gates = ids_ref[...], gates_ref[...]
    for r in range(2):
        G[e, x, pl.ds(r, 1), :] = jnp.sum(jnp.where(ids == 2 * t + r, gates, 0.0), axis=0, keepdims=True)
    pl.semaphore_wait(barrier, len(peers))

    for k, d in enumerate((1, 3, 2)):
        dst = slab(y, x)
        for i, (src, to) in enumerate(
            (
                (wi_ref.at[:, rows(at_x(d)), :], W.at[0:2, :, dst]),
                (vi_ref.at[:, rows(at_x(d)), :], W.at[2:4, :, dst]),
                (wo_ref.at[rows(at_x(d)), :], W.at[4, :, dst]),
                (vo_ref.at[rows(at_x(d)), :], W.at[5, :, dst]),
            )
        ):
            send(src, to, wa_s.at[k, i], wa_r.at[k, i], dev_x(d))
    for k, d in enumerate((1, 3, 2)):
        send(G.at[e, x], G.at[e, x], g_s.at[k], g_r.at[k], dev_x(d))
    for copy in mine:
        copy.wait()

    def xhalf(a, core, h):
        return X.at[:, a, core, pl.ds(h * half, half), :]

    send(xhalf(x, e, 0), xhalf(x, e, 0), xh_s.at[0, 0], xh_r.at[0, 0], dev_x(1))
    send(xhalf(x, e, 1), xhalf(x, e, 1), xh_s.at[1, 1], xh_r.at[1, 1], dev_x(3))
    send(xhalf(x, e, 1), xhalf(x, e, 1), xh_s.at[0, 1], xh_r.at[0, 1], dev_x(1))
    send(xhalf(x, e, 0), xhalf(x, e, 0), xh_s.at[1, 0], xh_r.at[1, 0], dev_x(3))
    for h in range(2):
        send(xhalf(x, e, h), xhalf(x, e, h), dd_s.at[0, h], dd_r.at[0, h], partner)

    def wslab(yy, d):
        return W.at[:, :, slab(yy, at_x(SIDE - d))]

    def whalf(yy, d, h):
        return W.at[3 * h : 3 * h + 3, :, slab(yy, at_x(SIDE - d))]

    order = (0, 1, 3, 2)
    for k, d in enumerate(order):
        if d:
            i = (1, 3, 2).index(d)
            src = slab(y, at_x(SIDE - d))
            for j, to in enumerate((W.at[0:2, :, src], W.at[2:4, :, src], W.at[4, :, src], W.at[5, :, src])):
                got(to, wa_s.at[i, j], wa_r.at[i, j])
        send(wslab(y, d), wslab(y, d), wy_s.at[0, k], wy_r.at[0, k], dev_y(1))
        send(wslab(y, d), wslab(y, d), wy_s.at[1, k], wy_r.at[1, k], dev_y(3))
    for k, d in enumerate(order):
        got(wslab(at_y(3), d), wy_s.at[0, k], wy_r.at[0, k])
        send(whalf(at_y(3), d, 0), whalf(at_y(3), d, 0), wf_s.at[0, k], wf_r.at[0, k], dev_y(1))
        got(wslab(at_y(1), d), wy_s.at[1, k], wy_r.at[1, k])
        send(whalf(at_y(1), d, 1), whalf(at_y(1), d, 1), wf_s.at[1, k], wf_r.at[1, k], dev_y(3))

    for k, d in enumerate((1, 3, 2)):
        src = at_x(SIDE - d)
        got(G.at[e, src], g_s.at[k], g_r.at[k])
    send(G.at[e], G.at[e], gd.at[0], gd.at[1], partner)

    got(xhalf(at_x(3), e, 0), xh_s.at[0, 0], xh_r.at[0, 0])
    send(xhalf(at_x(3), e, 0), xhalf(at_x(3), e, 0), xf_s.at[0], xf_r.at[0], dev_x(1))
    send(xhalf(at_x(3), e, 0), xhalf(at_x(3), e, 0), dd_s.at[1, 0], dd_r.at[1, 0], partner)
    got(xhalf(at_x(1), e, 1), xh_s.at[1, 1], xh_r.at[1, 1])
    send(xhalf(at_x(1), e, 1), xhalf(at_x(1), e, 1), xf_s.at[1], xf_r.at[1], dev_x(3))
    send(xhalf(at_x(1), e, 1), xhalf(at_x(1), e, 1), dd_s.at[3, 1], dd_r.at[3, 1], partner)

    for k, d in enumerate(order):
        got(whalf(at_y(2), d, 0), wf_s.at[0, k], wf_r.at[0, k])
        got(whalf(at_y(2), d, 1), wf_s.at[1, k], wf_r.at[1, k])
    got(G.at[1 - e], gd.at[0], gd.at[1])

    n_acc = acc.shape[1]
    cut = n_acc // 2
    step = 32

    def group(a, rel, first):
        def both(i, cols=slice(None)):
            v = X[i, a, :, :, cols]
            return v.reshape(2 * tok, v.shape[-1])

        C[0 : 2 * q, :] = mm(W[0:2].reshape(2 * q, width), both(0), NT)
        C[2 * q : 4 * q, :] = mm(W[2:4].reshape(2 * q, width), both(0), NT)
        C[4 * q : 6 * q, :] = mm(W[0:2].reshape(2 * q, width), both(1), NT)
        C[6 * q : 8 * q, :] = mm(W[4:6].reshape(2 * q, width), both(2), NT)
        gate = jnp.concatenate([G[0, a, pl.ds(e, 1), :], G[1, a, pl.ds(e, 1), :]], axis=1)

        def rows_of(i, carry):
            at = pl.multiple_of(i * step, step)

            def c(k):
                return C[pl.ds(k * q + at, step), :]

            pre, up = c(0), c(1)
            pre_dot, up_dot = c(4) + c(2), c(5) + c(3)
            g, g_dot = c(6) * gate, c(7) * gate
            sigma = jax.nn.sigmoid(pre)
            rest = 1.0 - sigma
            s0 = pre * sigma
            s1 = sigma * (1.0 + pre * rest)
            s2 = sigma * rest * (2.0 + pre * (1.0 - 2.0 * sigma))
            S[pl.ds(at, step), :] = (
                g_dot * up * s1 + g * up_dot * s1 + g * up * s2 * pre_dot
            ).astype(BF16)
            S[pl.ds(q + at, step), :] = (g_dot * s0 + g * s1 * pre_dot).astype(BF16)
            S[pl.ds(2 * q + at, step), :] = (g * up * s1).astype(BF16)
            S[pl.ds(3 * q + at, step), :] = (g * s0).astype(BF16)
            H[pl.ds(at, step), :] = ((s1 * pre_dot * up + s0 * up_dot) * gate).astype(BF16)
            return carry

        lax.fori_loop(0, q // step, rows_of, 0)
        ST[...] = S[...].T

        def columns(n, carry):
            cols = pl.ds(pl.multiple_of(n * part, part), part)
            value = mm(ST[...], W[0:4, :, cols].reshape(4 * q, part))
            for core in range(2):

                @pl.when(e == core)
                def _():
                    Pown[rel, :, cols] = value[core * tok : (core + 1) * tok]
                    PDs[rel, :, cols] = value[(1 - core) * tok : (2 - core) * tok].astype(BF16)

            w_in = mm(S[2 * q : 4 * q, :], both(1, cols)) + mm(S[0 : 2 * q, :], both(0, cols))
            w_out = mm(H[...], both(2, cols))
            if first:
                acc[n, 0 : 2 * q, :] = w_in
                acc[n, 2 * q : 3 * q, :] = w_out
            else:
                acc[n, 0 : 2 * q, :] += w_in
                acc[n, 2 * q : 3 * q, :] += w_out
            return carry

        lax.fori_loop(0, SIDE, columns, 0)
        send(PDs.at[rel], PDr.at[rel], pd_s.at[rel], pd_r.at[rel], partner)

    def summed(rel, h):
        at = pl.ds(h * half, half)
        return Pown[rel, at, :] + PDr[rel, at, :].astype(F32)

    for h in range(2):
        got(xhalf(x, 1 - e, h), dd_s.at[0, h], dd_r.at[0, h])
    group(x, 0, True)

    got(xhalf(at_x(3), e, 1), xh_s.at[0, 1], xh_r.at[0, 1])
    send(xhalf(at_x(3), e, 1), xhalf(at_x(3), e, 1), dd_s.at[1, 1], dd_r.at[1, 1], partner)
    got(xhalf(at_x(1), e, 0), xh_s.at[1, 0], xh_r.at[1, 0])
    send(xhalf(at_x(1), e, 0), xhalf(at_x(1), e, 0), dd_s.at[3, 0], dd_r.at[3, 0], partner)
    for h in range(2):
        got(xhalf(at_x(3), 1 - e, h), dd_s.at[1, h], dd_r.at[1, h])
    group(at_x(3), 1, False)

    got(xhalf(at_x(2), e, 0), xf_s.at[0], xf_r.at[0])
    send(xhalf(at_x(2), e, 0), xhalf(at_x(2), e, 0), dd_s.at[2, 0], dd_r.at[2, 0], partner)
    got(xhalf(at_x(2), e, 1), xf_s.at[1], xf_r.at[1])
    send(xhalf(at_x(2), e, 1), xhalf(at_x(2), e, 1), dd_s.at[2, 1], dd_r.at[2, 1], partner)
    for h in range(2):
        got(xhalf(at_x(1), 1 - e, h), dd_s.at[3, h], dd_r.at[3, h])
    group(at_x(1), 3, False)

    for h in range(2):
        got(xhalf(at_x(2), 1 - e, h), dd_s.at[2, h], dd_r.at[2, h])
    group(at_x(2), 2, False)

    def acc_half(k, h):
        return acc[k, h * cut : (h + 1) * cut, :]

    for h in range(2):
        yopp[h] = acc_half(at_y(2), h).astype(BF16)
        send(yopp.at[h], yropp.at[h], yo_s.at[h], yo_r.at[h], dev_y(1 + 2 * h))
    ys[0, 1] = acc_half(at_y(1), 1).astype(BF16)
    send(ys.at[0, 1], yr.at[0, 1], yp_s.at[0, 1], yp_r.at[0, 1], dev_y(1))
    ys[1, 0] = acc_half(at_y(3), 0).astype(BF16)
    send(ys.at[1, 0], yr.at[1, 0], yp_s.at[1, 0], yp_r.at[1, 0], dev_y(3))

    for rel in (0, 1, 3, 2):
        got(PDr.at[rel], pd_s.at[rel], pd_r.at[rel])
    for h in range(2):
        xopp[h] = summed(2, h).astype(BF16)
        send(xopp.at[h], xropp.at[h], xo_s.at[h], xo_r.at[h], dev_x(1 + 2 * h))
    xs[0, 1] = summed(3, 1).astype(BF16)
    send(xs.at[0, 1], xr.at[0, 1], xp_s.at[0, 1], xp_r.at[0, 1], dev_x(1))
    xs[1, 0] = summed(1, 0).astype(BF16)
    send(xs.at[1, 0], xr.at[1, 0], xp_s.at[1, 0], xp_r.at[1, 0], dev_x(3))

    got(xropp.at[0], xo_s.at[0], xo_r.at[0])
    xs[0, 0] = (summed(3, 0) + xropp[0].astype(F32)).astype(BF16)
    send(xs.at[0, 0], xr.at[0, 0], xp_s.at[0, 0], xp_r.at[0, 0], dev_x(1))
    got(xropp.at[1], xo_s.at[1], xo_r.at[1])
    xs[1, 1] = (summed(1, 1) + xropp[1].astype(F32)).astype(BF16)
    send(xs.at[1, 1], xr.at[1, 1], xp_s.at[1, 1], xp_r.at[1, 1], dev_x(3))

    got(yropp.at[0], yo_s.at[0], yo_r.at[0])
    ys[0, 0] = (acc_half(at_y(1), 0) + yropp[0].astype(F32)).astype(BF16)
    send(ys.at[0, 0], yr.at[0, 0], yp_s.at[0, 0], yp_r.at[0, 0], dev_y(1))
    got(yropp.at[1], yo_s.at[1], yo_r.at[1])
    ys[1, 1] = (acc_half(at_y(3), 1) + yropp[1].astype(F32)).astype(BF16)
    send(ys.at[1, 1], yr.at[1, 1], yp_s.at[1, 1], yp_r.at[1, 1], dev_y(3))

    piece = tok // n_z
    for h in (1, 0):
        got(xr.at[0, h], xp_s.at[0, h], xp_r.at[0, h])
        got(xr.at[1, h], xp_s.at[1, h], xp_r.at[1, h])
        total = summed(0, h) + xr[0, h].astype(F32) + xr[1, h].astype(F32)
        at = pl.ds(h * (n_z // 2), n_z // 2)
        Zs[at] = total.reshape(n_z // 2, piece, width).astype(BF16)
    Zr[t] = Zs[t]
    for d in range(1, n_z):
        send(Zs.at[lax.rem(t + d, n_z)], Zr.at[t], z1_s.at[d - 1], z1_r.at[d - 1], dev_z(d))

    total = []
    for h in range(2):
        got(yr.at[0, h], yp_s.at[0, h], yp_r.at[0, h])
        got(yr.at[1, h], yp_s.at[1, h], yp_r.at[1, h])
        value = acc_half(y, h) + yr[0, h].astype(F32) + yr[1, h].astype(F32)
        value = value.astype(BF16)
        for k in range(SIDE):
            R[k, h * cut : (h + 1) * cut, :] = value[:, k * lanes : (k + 1) * lanes]
    OUT[x] = R[x]
    for k, d in enumerate((1, 3, 2)):
        send(R.at[at_x(d)], OUT.at[x], ra_s.at[k], ra_r.at[k], dev_x(d))

    for d in range(1, n_z):
        got(Zr.at[lax.rem(t + n_z - d, n_z)], z1_s.at[d - 1], z1_r.at[d - 1])
    done = Zr[0].astype(F32)
    for k in range(1, n_z):
        done += Zr[k].astype(F32)
    Zf[t] = done.astype(BF16)
    for d in range(1, n_z):
        send(Zf.at[t], Zf.at[t], z2_s.at[d - 1], z2_r.at[d - 1], dev_z(d))

    for k, d in enumerate((1, 3, 2)):
        got(OUT.at[at_x(SIDE - d)], ra_s.at[k], ra_r.at[k])
    for k in range(SIDE):
        at = slice(k * q, (k + 1) * q)
        for i in range(2):
            out_in[i, at, :] = OUT[k, i * q : (i + 1) * q, :].astype(F32)
        out_out[at, :] = OUT[k, 2 * q : 3 * q, :].astype(F32)

    for d in range(1, n_z):
        got(Zf.at[lax.rem(t + n_z - d, n_z)], z2_s.at[d - 1], z2_r.at[d - 1])
    out_tok[...] = Zf[...].astype(F32).reshape(tok, width)
    for copy in pending:
        copy.wait_send()


def shards(n_z, tokens, tangent, cotangent, expert_ids, gates, w_in, v_in, w_out, v_out):
    tok = tokens.shape[0]
    ff, lanes = w_in.shape[2:]
    width = tokens.shape[1]
    q = ff // SIDE
    half = tok // 2
    part = width // SIDE
    cut = 3 * q // 2
    dma = pltpu.SemaphoreType.DMA
    vmem = pl.BlockSpec(memory_space=pltpu.VMEM)
    hbm = pl.BlockSpec(memory_space=pltpu.HBM)
    y_tok, y_in, y_out = pl.pallas_call(
        functools.partial(kernel, n_z),
        out_shape=(
            jax.ShapeDtypeStruct((tok, width), F32),
            jax.ShapeDtypeStruct((2, ff, lanes), F32),
            jax.ShapeDtypeStruct((ff, lanes), F32),
        ),
        in_specs=[vmem, vmem] + [hbm] * 7,
        out_specs=(vmem, vmem, vmem),
        scratch_shapes=[
            pltpu.VMEM((6, q, width), BF16),
            pltpu.VMEM((3, SIDE, 2, tok, width), BF16),
            pltpu.VMEM((2, SIDE, 8, tok), F32),
            pltpu.VMEM((8 * q, 2 * tok), F32),
            pltpu.VMEM((4 * q, 2 * tok), BF16),
            pltpu.VMEM((2 * tok, 4 * q), BF16),
            pltpu.VMEM((q, 2 * tok), BF16),
            pltpu.VMEM((SIDE, 3 * q, part), F32),
            pltpu.VMEM((4, tok, width), F32),
            pltpu.VMEM((4, tok, width), BF16),
            pltpu.VMEM((4, tok, width), BF16),
            pltpu.VMEM((2, 2, half, width), BF16),
            pltpu.VMEM((2, half, width), BF16),
            pltpu.VMEM((2, 2, half, width), BF16),
            pltpu.VMEM((2, half, width), BF16),
            pltpu.VMEM((2, 2, cut, part), BF16),
            pltpu.VMEM((2, cut, part), BF16),
            pltpu.VMEM((2, 2, cut, part), BF16),
            pltpu.VMEM((2, cut, part), BF16),
            pltpu.VMEM((SIDE, 3 * q, lanes), BF16),
            pltpu.VMEM((SIDE, 3 * q, lanes), BF16),
            pltpu.VMEM((n_z, tok // n_z, width), BF16),
            pltpu.VMEM((n_z, tok // n_z, width), BF16),
            pltpu.VMEM((n_z, tok // n_z, width), BF16),
            dma((7,)),
            dma((3, 4)), dma((3, 4)),
            dma((2, 4)), dma((2, 4)),
            dma((2, 4)), dma((2, 4)),
            dma((2, 2)), dma((2, 2)),
            dma((2,)), dma((2,)),
            dma((3,)), dma((3,)),
            dma((2,)),
            dma((4, 2)), dma((4, 2)),
            dma((4,)), dma((4,)),
            dma((2,)), dma((2,)),
            dma((2, 2)), dma((2, 2)),
            dma((2,)), dma((2,)),
            dma((2, 2)), dma((2, 2)),
            dma((3,)), dma((3,)),
            dma((n_z - 1,)), dma((n_z - 1,)),
            dma((n_z - 1,)), dma((n_z - 1,)),
        ],
        compiler_params=pltpu.CompilerParams(
            collective_id=0, has_side_effects=True, vmem_limit_bytes=62 * 1024 * 1024
        ),
    )(
        expert_ids.T, gates.T, tokens, tangent, cotangent, w_in[0], v_in[0], w_out[0], v_out[0]
    )
    return y_tok, y_in[None], y_out[None]


def solution(mesh):
    rows = P(("expert", "dp"), None)
    w_spec = P(("tensor", "expert"), None, None, "dp")
    o_spec = P(("tensor", "expert"), None, "dp")
    return jax.shard_map(
        functools.partial(shards, mesh.shape["tensor"]),
        mesh=mesh,
        in_specs=(rows,) * 5 + (w_spec, w_spec, o_spec, o_spec),
        out_specs=(rows, w_spec, o_spec),
        check_vma=False,
    )
```

profile of v0, /device:TPU:24, one launch (start us, length us, event | category | flops | bytes accessed | tf_op | source)
XLA Modules:
  0.0 141.0 jit_solution(16928983378878743995)
XLA Ops:
  0.6 136.0 %shard_map.112 = (f32[128,2048]{1,0:T(8,128)}, f32[2,768,128]{2,1,0:T(8,128)}, f32[768,128]{1,0:T(8,128)}) custom-call(s32[8,128]{1,0:T(8,128)} %bitcast.14, f32[8,128]{1,0:T(8,128)} %bitcast.15, bf16[128,2048]{1,0:T(8,128)(2,1)} %tok_ref.1, bf16[128,2048]{1,0:T(8,128)(2,1)} %tan_ref.1, bf16[128,2048]{1,0:T(8,128)(2,1)} %cot_ref.1, ...), custom_call_target="tpu_custom_call" | custom-call | tf_op jit(solution)/shard_map/pallas_call | solution.py:346
  136.6 0.0 copy-start
  136.6 2.4 %copy.15 = f32[128,2048]{1,0:T(8,128)} copy(f32[128,2048]{1,0:T(8,128)} %get-tuple-element.12) | data formatting | bytes 2097152
  139.0 0.0 copy-done
  139.0 0.0 copy-start.1
  139.0 0.9 copy.16
  139.9 0.4 copy-done.1
  140.2 0.7 copy.17
Async XLA Ops:
  136.6 2.4 %copy-start = (f32[2,768,128]{2,1,0:T(8,128)S(1)}, f32[2,768,128]{2,1,0:T(8,128)}, u32[]{:S(2)}) copy-start(f32[2,768,128]{2,1,0:T(8,128)} %get-tuple-element.7) | copy-start | bytes 2359300
  139.0 1.2 copy-start.1
where the time goes:
time: 142 us; the launch traced here: 141 us
  Pallas kernels  136 us (96%)
  local copies, waits for them, and re-layouts  4.35 us (3%)
    pallas_call x1, Pallas kernels, shards(): pl.pallas_call(functools.partial(kernel, n_z), out_shape=(jax.ShapeDtypeS...  136 us
    unnamed x7, local copies, waits for them, and re-layouts  4.35 us

commit v1 on v0

v1 whole, which is shorter than its diff:
```python
import functools

import jax
import jax.numpy as jnp
from jax import lax
from jax.experimental import pallas as pl
from jax.experimental.pallas import tpu as pltpu
from jax.sharding import PartitionSpec as P

MESH = pl.DeviceIdType.MESH
F32 = jnp.float32
BF16 = jnp.bfloat16
SIDE = 4
NT = (((1,), (1,)), ((), ()))
NN = (((1,), (0,)), ((), ()))


def mm(a, b, dims=NN):
    return lax.dot_general(a, b, dims, preferred_element_type=F32)


def kernel(
    n_z, ids_ref, gates_ref, tok_ref, tan_ref, cot_ref, wi_ref, vi_ref, wo_ref, vo_ref,
    out_tok, out_in, out_out,
    W, stage, X, G, C, S, ST, H, acc, Pown, PDs, PDr, xs, xopp, xr, xropp, ys, yopp, yr, yropp, R, OUT, Zs, Zr, Zf,
    loc, wa_s, wa_r, st_s, st_r, sf_s, sf_r, wy_s, wy_r, wf_s, wf_r, xh_s, xh_r, xf_s, xf_r, zx_s, zx_r,
    g_s, g_r, gd, dd_s, dd_r, pd_s, pd_r,
    xo_s, xo_r, xp_s, xp_r, yo_s, yo_r, yp_s, yp_r, ra_s, ra_r, z1_s, z1_r, z2_s, z2_r,
):
    t = lax.axis_index("tensor")
    e = lax.axis_index("expert")
    p = lax.axis_index("dp")
    y, x = p // SIDE, p % SIDE
    color = lax.rem(t, 2)
    tok = tok_ref.shape[0]
    half = tok // 2
    quarter = tok // 4
    lanes = wi_ref.shape[-1]
    q = W.shape[1]
    width = W.shape[2]
    part = width // SIDE

    def at_x(d):
        return lax.rem(x + d, SIDE)

    def at_y(d):
        return lax.rem(y + d, SIDE)

    def dev_x(d):
        return (t, e, y * SIDE + at_x(d))

    def dev_y(d):
        return (t, e, at_y(d) * SIDE + x)

    def dev_z(d):
        return (lax.rem(t + d, n_z), e, p)

    partner = (t, 1 - e, p)
    pending = []

    def send(src, dst, ssem, rsem, dev):
        copy = pltpu.make_async_remote_copy(
            src_ref=src, dst_ref=dst, send_sem=ssem, recv_sem=rsem, device_id=dev, device_id_type=MESH
        )
        copy.start()
        pending.append(copy)

    def got(dst, ssem, rsem):
        pltpu.make_async_remote_copy(
            src_ref=dst, dst_ref=dst, send_sem=ssem, recv_sem=rsem, device_id=partner, device_id_type=MESH
        ).wait_recv()

    barrier = pltpu.get_barrier_semaphore()
    peers = [partner] + [dev_x(d) for d in (1, 2, 3)] + [dev_y(d) for d in (1, 3)] + [dev_z(d) for d in range(1, n_z)]
    for peer in peers:
        pl.semaphore_signal(barrier, inc=1, device_id=peer, device_id_type=MESH)

    def slab(yy, xx):
        return pl.ds(pl.multiple_of((yy * SIDE + xx) * lanes, lanes), lanes)

    def rows(k):
        return pl.ds(pl.multiple_of(k * q, q), q)

    mine = [
        pltpu.make_async_copy(wi_ref.at[:, rows(x), :], W.at[0:2, :, slab(y, x)], loc.at[3]),
        pltpu.make_async_copy(vi_ref.at[:, rows(x), :], W.at[2:4, :, slab(y, x)], loc.at[4]),
        pltpu.make_async_copy(wo_ref.at[rows(x), :], W.at[4, :, slab(y, x)], loc.at[5]),
        pltpu.make_async_copy(vo_ref.at[rows(x), :], W.at[5, :, slab(y, x)], loc.at[6]),
        pltpu.make_async_copy(tok_ref, X.at[0, x, e], loc.at[0]),
        pltpu.make_async_copy(tan_ref, X.at[1, x, e], loc.at[1]),
        pltpu.make_async_copy(cot_ref, X.at[2, x, e], loc.at[2]),
    ]
    for copy in mine:
        copy.start()
    ids, gates = ids_ref[...], gates_ref[...]
    for r in range(2):
        G[e, x, pl.ds(r, 1), :] = jnp.sum(jnp.where(ids == 2 * t + r, gates, 0.0), axis=0, keepdims=True)
    pl.semaphore_wait(barrier, len(peers))

    def thirds(buf, h):
        return (buf.at[h, 0:2], buf.at[h, 2])

    def in_w(h, at):
        return (W.at[2 * h : 2 * h + 2, :, at], W.at[4 + h, :, at])

    def from_args(h, k):
        return ((wi_ref, vi_ref)[h].at[:, rows(k), :], (wo_ref, vo_ref)[h].at[rows(k), :])

    for h in range(2):
        for i, (src, to) in enumerate(zip(from_args(h, at_x(2)), thirds(stage, h))):
            send(src, to, st_s.at[h, i], st_r.at[h, i], dev_x(1 + 2 * h))
    for k, d in enumerate((1, 3)):
        for h in range(2):
            for i, (src, to) in enumerate(zip(from_args(h, at_x(d)), in_w(h, slab(y, x)))):
                send(src, to, wa_s.at[k, 2 * h + i], wa_r.at[k, 2 * h + i], dev_x(d))
    for k, d in enumerate((1, 3, 2)):
        send(G.at[e, x], G.at[e, x], g_s.at[k], g_r.at[k], dev_x(d))
    for copy in mine:
        copy.wait()

    def wslab(yy, d):
        return W.at[:, :, slab(yy, at_x(SIDE - d))]

    def whalf(yy, d, h):
        return W.at[3 * h : 3 * h + 3, :, slab(yy, at_x(SIDE - d))]

    order = (0, 1, 3, 2)

    def spread(d):
        k = order.index(d)
        send(wslab(y, d), wslab(y, d), wy_s.at[0, k], wy_r.at[0, k], dev_y(1))
        send(wslab(y, d), wslab(y, d), wy_s.at[1, k], wy_r.at[1, k], dev_y(3))

    def onward(d):
        k = order.index(d)
        got(wslab(at_y(3), d), wy_s.at[0, k], wy_r.at[0, k])
        send(whalf(at_y(3), d, 0), whalf(at_y(3), d, 0), wf_s.at[0, k], wf_r.at[0, k], dev_y(1))
        got(wslab(at_y(1), d), wy_s.at[1, k], wy_r.at[1, k])
        send(whalf(at_y(1), d, 1), whalf(at_y(1), d, 1), wf_s.at[1, k], wf_r.at[1, k], dev_y(3))

    spread(0)
    send(X.at[:, x, e], X.at[:, x, e], dd_s.at[0, 0, 0], dd_r.at[0, 0, 0], partner)
    for h in range(2):
        for i, to in enumerate(thirds(stage, h)):
            got(to, st_s.at[h, i], st_r.at[h, i])
        for i, (src, to) in enumerate(zip(thirds(stage, h), in_w(h, slab(y, at_x(3 - 2 * h))))):
            send(src, to, sf_s.at[h, i], sf_r.at[h, i], dev_x(1 + 2 * h))

    def piece(a, own, h, core):
        first = (color if own else 1 - color) * half + h * quarter
        return X.at[:, a, core, pl.ds(pl.multiple_of(first, quarter), quarter), :]

    for k, h in ((0, 0), (1, 1), (0, 1), (1, 0)):
        part_of = piece(x, True, h, e)
        send(part_of, part_of, xh_s.at[k, h], xh_r.at[k, h], dev_x(1 + 2 * k))

    def to_core(rel, own, h):
        part_of = piece(at_x(SIDE - rel), own, h, e)
        k = 0 if own else 1
        send(part_of, part_of, dd_s.at[rel, k, h], dd_r.at[rel, k, h], partner)

    def to_planes(rel, h):
        part_of = piece(at_x(SIDE - rel), True, h, e)
        send(part_of, part_of, zx_s.at[rel - 1, h], zx_r.at[rel - 1, h], dev_z(1 if h == 0 else n_z - 1))

    def over_x(rel, h):
        a = at_x(SIDE - rel)
        if rel == 2:
            got(piece(a, True, h, e), xf_s.at[h], xf_r.at[h])
        else:
            k = 0 if rel == 1 else 1
            got(piece(a, True, h, e), xh_s.at[k, h], xh_r.at[k, h])
            if h == k:
                send(piece(a, True, h, e), piece(a, True, h, e), xf_s.at[h], xf_r.at[h], dev_x(1 + 2 * k))
        to_planes(rel, h)
        to_core(rel, True, h)

    def over_z(rel, h):
        got(piece(at_x(SIDE - rel), False, h, e), zx_s.at[rel - 1, h], zx_r.at[rel - 1, h])
        to_core(rel, False, h)

    for k, d in enumerate((1, 3)):
        for h in range(2):
            for i, to in enumerate(in_w(h, slab(y, at_x(SIDE - d)))):
                got(to, wa_s.at[k, 2 * h + i], wa_r.at[k, 2 * h + i])
        spread(d)
    for h in range(2):
        for i, to in enumerate(in_w(h, slab(y, at_x(2)))):
            got(to, sf_s.at[h, i], sf_r.at[h, i])
    spread(2)
    onward(0)
    onward(1)
    over_x(1, 0)
    over_x(3, 1)
    onward(3)
    onward(2)
    for k, d in enumerate((1, 3, 2)):
        got(G.at[e, at_x(SIDE - d)], g_s.at[k], g_r.at[k])
    send(G.at[e], G.at[e], gd.at[0], gd.at[1], partner)
    over_x(1, 1)
    over_x(3, 0)
    over_z(1, 0)
    over_z(3, 1)
    over_x(2, 0)
    over_x(2, 1)
    over_z(3, 0)
    over_z(1, 1)
    for k, d in enumerate(order):
        got(whalf(at_y(2), d, 0), wf_s.at[0, k], wf_r.at[0, k])
        got(whalf(at_y(2), d, 1), wf_s.at[1, k], wf_r.at[1, k])
    got(G.at[1 - e], gd.at[0], gd.at[1])

    n_acc = acc.shape[1]
    cut = n_acc // 2
    step = 32

    def tokens_of(a):
        return pl.ds(pl.multiple_of(a * 2 * tok, 2 * tok), 2 * tok)

    def forward(rel):
        a = at_x(SIDE - rel)
        if rel == 0:
            got(X.at[:, x, 1 - e], dd_s.at[0, 0, 0], dd_r.at[0, 0, 0])
        else:
            for k in range(2):
                for h in range(2):
                    got(piece(a, k == 0, h, 1 - e), dd_s.at[rel, k, h], dd_r.at[rel, k, h])

        def both(i):
            return X[i, a].reshape(2 * tok, width)

        C[0 : 2 * q, :] = mm(W[0:2].reshape(2 * q, width), both(0), NT)
        C[2 * q : 4 * q, :] = mm(W[2:4].reshape(2 * q, width), both(0), NT)
        C[4 * q : 6 * q, :] = mm(W[0:2].reshape(2 * q, width), both(1), NT)
        C[6 * q : 8 * q, :] = mm(W[4:6].reshape(2 * q, width), both(2), NT)
        gate = jnp.concatenate([G[0, a, pl.ds(e, 1), :], G[1, a, pl.ds(e, 1), :]], axis=1)
        cols = tokens_of(a)

        def rows_of(i, carry):
            at = pl.multiple_of(i * step, step)

            def c(k):
                return C[pl.ds(k * q + at, step), :]

            pre, up = c(0), c(1)
            pre_dot, up_dot = c(4) + c(2), c(5) + c(3)
            g, g_dot = c(6) * gate, c(7) * gate
            sigma = jax.nn.sigmoid(pre)
            rest = 1.0 - sigma
            s0 = pre * sigma
            s1 = sigma * (1.0 + pre * rest)
            s2 = sigma * rest * (2.0 + pre * (1.0 - 2.0 * sigma))
            S[pl.ds(at, step), cols] = (
                g_dot * up * s1 + g * up_dot * s1 + g * up * s2 * pre_dot
            ).astype(BF16)
            S[pl.ds(q + at, step), cols] = (g_dot * s0 + g * s1 * pre_dot).astype(BF16)
            S[pl.ds(2 * q + at, step), cols] = (g * up * s1).astype(BF16)
            S[pl.ds(3 * q + at, step), cols] = (g * s0).astype(BF16)
            H[pl.ds(at, step), cols] = ((s1 * pre_dot * up + s0 * up_dot) * gate).astype(BF16)
            return carry

        lax.fori_loop(0, q // step, rows_of, 0)

    def tokens_back(rel):
        ST[...] = S[:, tokens_of(at_x(SIDE - rel))].T

        def columns(n, carry):
            cols = pl.ds(pl.multiple_of(n * part, part), part)
            value = mm(ST[...], W[0:4, :, cols].reshape(4 * q, part))
            for core in range(2):

                @pl.when(e == core)
                def _():
                    Pown[rel, :, cols] = value[core * tok : (core + 1) * tok]
                    PDs[rel, :, cols] = value[(1 - core) * tok : (2 - core) * tok].astype(BF16)

            return carry

        lax.fori_loop(0, SIDE, columns, 0)
        send(PDs.at[rel], PDr.at[rel], pd_s.at[rel], pd_r.at[rel], partner)

    def weights_back(n):
        cols = pl.ds(pl.multiple_of(n * part, part), part)

        def every(i):
            return X[i, :, :, :, cols].reshape(SIDE * 2 * tok, part)

        acc[n, 0 : 2 * q, :] = mm(S[2 * q : 4 * q, :], every(1)) + mm(S[0 : 2 * q, :], every(0))
        acc[n, 2 * q : 3 * q, :] = mm(H[...], every(2))

    def summed(rel, h):
        at = pl.ds(h * half, half)
        return Pown[rel, at, :] + PDr[rel, at, :].astype(F32)

    def acc_half(k, h):
        return acc[k, h * cut : (h + 1) * cut, :]

    forward(0)
    forward(1)
    over_z(2, 0)
    over_z(2, 1)
    forward(3)
    forward(2)

    tokens_back(2)
    tokens_back(1)
    got(PDr.at[2], pd_s.at[2], pd_r.at[2])
    for h in range(2):
        xopp[h] = summed(2, h).astype(BF16)
        send(xopp.at[h], xropp.at[h], xo_s.at[h], xo_r.at[h], dev_x(1 + 2 * h))
    tokens_back(3)
    got(PDr.at[1], pd_s.at[1], pd_r.at[1])
    xs[1, 0] = summed(1, 0).astype(BF16)
    send(xs.at[1, 0], xr.at[1, 0], xp_s.at[1, 0], xp_r.at[1, 0], dev_x(3))
    weights_back(at_y(2))
    for h in range(2):
        yopp[h] = acc_half(at_y(2), h).astype(BF16)
        send(yopp.at[h], yropp.at[h], yo_s.at[h], yo_r.at[h], dev_y(1 + 2 * h))
    got(PDr.at[3], pd_s.at[3], pd_r.at[3])
    xs[0, 1] = summed(3, 1).astype(BF16)
    send(xs.at[0, 1], xr.at[0, 1], xp_s.at[0, 1], xp_r.at[0, 1], dev_x(1))
    weights_back(at_y(1))
    ys[0, 1] = acc_half(at_y(1), 1).astype(BF16)
    send(ys.at[0, 1], yr.at[0, 1], yp_s.at[0, 1], yp_r.at[0, 1], dev_y(1))
    weights_back(at_y(3))
    ys[1, 0] = acc_half(at_y(3), 0).astype(BF16)
    send(ys.at[1, 0], yr.at[1, 0], yp_s.at[1, 0], yp_r.at[1, 0], dev_y(3))
    tokens_back(0)

    got(xropp.at[0], xo_s.at[0], xo_r.at[0])
    xs[0, 0] = (summed(3, 0) + xropp[0].astype(F32)).astype(BF16)
    send(xs.at[0, 0], xr.at[0, 0], xp_s.at[0, 0], xp_r.at[0, 0], dev_x(1))
    got(xropp.at[1], xo_s.at[1], xo_r.at[1])
    xs[1, 1] = (summed(1, 1) + xropp[1].astype(F32)).astype(BF16)
    send(xs.at[1, 1], xr.at[1, 1], xp_s.at[1, 1], xp_r.at[1, 1], dev_x(3))
    weights_back(y)

    got(yropp.at[0], yo_s.at[0], yo_r.at[0])
    ys[0, 0] = (acc_half(at_y(1), 0) + yropp[0].astype(F32)).astype(BF16)
    send(ys.at[0, 0], yr.at[0, 0], yp_s.at[0, 0], yp_r.at[0, 0], dev_y(1))
    got(yropp.at[1], yo_s.at[1], yo_r.at[1])
    ys[1, 1] = (acc_half(at_y(3), 1) + yropp[1].astype(F32)).astype(BF16)
    send(ys.at[1, 1], yr.at[1, 1], yp_s.at[1, 1], yp_r.at[1, 1], dev_y(3))

    piece_z = tok // n_z
    got(PDr.at[0], pd_s.at[0], pd_r.at[0])
    for h in (1, 0):
        got(xr.at[0, h], xp_s.at[0, h], xp_r.at[0, h])
        got(xr.at[1, h], xp_s.at[1, h], xp_r.at[1, h])
        total = summed(0, h) + xr[0, h].astype(F32) + xr[1, h].astype(F32)
        at = pl.ds(h * (n_z // 2), n_z // 2)
        Zs[at] = total.reshape(n_z // 2, piece_z, width).astype(BF16)
    Zr[t] = Zs[t]
    for d in range(1, n_z):
        send(Zs.at[lax.rem(t + d, n_z)], Zr.at[t], z1_s.at[d - 1], z1_r.at[d - 1], dev_z(d))

    for h in range(2):
        got(yr.at[0, h], yp_s.at[0, h], yp_r.at[0, h])
        got(yr.at[1, h], yp_s.at[1, h], yp_r.at[1, h])
        value = acc_half(y, h) + yr[0, h].astype(F32) + yr[1, h].astype(F32)
        value = value.astype(BF16)
        for k in range(SIDE):
            R[k, h * cut : (h + 1) * cut, :] = value[:, k * lanes : (k + 1) * lanes]
    OUT[x] = R[x]
    for k, d in enumerate((1, 3, 2)):
        send(R.at[at_x(d)], OUT.at[x], ra_s.at[k], ra_r.at[k], dev_x(d))

    for d in range(1, n_z):
        got(Zr.at[lax.rem(t + n_z - d, n_z)], z1_s.at[d - 1], z1_r.at[d - 1])
    done = Zr[0].astype(F32)
    for k in range(1, n_z):
        done += Zr[k].astype(F32)
    Zf[t] = done.astype(BF16)
    for d in range(1, n_z):
        send(Zf.at[t], Zf.at[t], z2_s.at[d - 1], z2_r.at[d - 1], dev_z(d))

    for k, d in enumerate((1, 3, 2)):
        got(OUT.at[at_x(SIDE - d)], ra_s.at[k], ra_r.at[k])
    for k in range(SIDE):
        at = slice(k * q, (k + 1) * q)
        for i in range(2):
            out_in[i, at, :] = OUT[k, i * q : (i + 1) * q, :]
        out_out[at, :] = OUT[k, 2 * q : 3 * q, :]

    for d in range(1, n_z):
        got(Zf.at[lax.rem(t + n_z - d, n_z)], z2_s.at[d - 1], z2_r.at[d - 1])
    out_tok[...] = Zf[...].reshape(tok, width)
    for copy in pending:
        copy.wait_send()


def shards(n_z, tokens, tangent, cotangent, expert_ids, gates, w_in, v_in, w_out, v_out):
    tok = tokens.shape[0]
    ff, lanes = w_in.shape[2:]
    width = tokens.shape[1]
    q = ff // SIDE
    half = tok // 2
    part = width // SIDE
    cut = 3 * q // 2
    dma = pltpu.SemaphoreType.DMA
    vmem = pl.BlockSpec(memory_space=pltpu.VMEM)
    hbm = pl.BlockSpec(memory_space=pltpu.HBM)
    y_tok, y_in, y_out = pl.pallas_call(
        functools.partial(kernel, n_z),
        out_shape=(
            jax.ShapeDtypeStruct((tok, width), BF16),
            jax.ShapeDtypeStruct((2, ff, lanes), BF16),
            jax.ShapeDtypeStruct((ff, lanes), BF16),
        ),
        in_specs=[vmem, vmem] + [hbm] * 7,
        out_specs=(vmem, vmem, vmem),
        scratch_shapes=[
            pltpu.VMEM((6, q, width), BF16),
            pltpu.VMEM((2, 3, q, lanes), BF16),
            pltpu.VMEM((3, SIDE, 2, tok, width), BF16),
            pltpu.VMEM((2, SIDE, 8, tok), F32),
            pltpu.VMEM((8 * q, 2 * tok), F32),
            pltpu.VMEM((4 * q, SIDE * 2 * tok), BF16),
            pltpu.VMEM((2 * tok, 4 * q), BF16),
            pltpu.VMEM((q, SIDE * 2 * tok), BF16),
            pltpu.VMEM((SIDE, 3 * q, part), F32),
            pltpu.VMEM((4, tok, width), F32),
            pltpu.VMEM((4, tok, width), BF16),
            pltpu.VMEM((4, tok, width), BF16),
            pltpu.VMEM((2, 2, half, width), BF16),
            pltpu.VMEM((2, half, width), BF16),
            pltpu.VMEM((2, 2, half, width), BF16),
            pltpu.VMEM((2, half, width), BF16),
            pltpu.VMEM((2, 2, cut, part), BF16),
            pltpu.VMEM((2, cut, part), BF16),
            pltpu.VMEM((2, 2, cut, part), BF16),
            pltpu.VMEM((2, cut, part), BF16),
            pltpu.VMEM((SIDE, 3 * q, lanes), BF16),
            pltpu.VMEM((SIDE, 3 * q, lanes), BF16),
            pltpu.VMEM((n_z, tok // n_z, width), BF16),
            pltpu.VMEM((n_z, tok // n_z, width), BF16),
            pltpu.VMEM((n_z, tok // n_z, width), BF16),
            dma((7,)),
            dma((2, 4)), dma((2, 4)),
            dma((2, 2)), dma((2, 2)),
            dma((2, 2)), dma((2, 2)),
            dma((2, 4)), dma((2, 4)),
            dma((2, 4)), dma((2, 4)),
            dma((2, 2)), dma((2, 2)),
            dma((2,)), dma((2,)),
            dma((3, 2)), dma((3, 2)),
            dma((3,)), dma((3,)),
            dma((2,)),
            dma((4, 2, 2)), dma((4, 2, 2)),
            dma((4,)), dma((4,)),
            dma((2,)), dma((2,)),
            dma((2, 2)), dma((2, 2)),
            dma((2,)), dma((2,)),
            dma((2, 2)), dma((2, 2)),
            dma((3,)), dma((3,)),
            dma((n_z - 1,)), dma((n_z - 1,)),
            dma((n_z - 1,)), dma((n_z - 1,)),
        ],
        compiler_params=pltpu.CompilerParams(
            collective_id=0, has_side_effects=True, vmem_limit_bytes=62 * 1024 * 1024
        ),
    )(
        expert_ids.T, gates.T, tokens, tangent, cotangent, w_in[0], v_in[0], w_out[0], v_out[0]
    )
    return y_tok.astype(F32), y_in[None].astype(F32), y_out[None].astype(F32)


def solution(mesh):
    rows = P(("expert", "dp"), None)
    w_spec = P(("tensor", "expert"), None, None, "dp")
    o_spec = P(("tensor", "expert"), None, "dp")
    return jax.shard_map(
        functools.partial(shards, mesh.shape["tensor"]),
        mesh=mesh,
        in_specs=(rows,) * 5 + (w_spec, w_spec, o_spec, o_spec),
        out_specs=(rows, w_spec, o_spec),
        check_vma=False,
    )
```

time: 142 us -> 122 us (0.86)
  the two profiles are of different devices: /device:TPU:24 before, /device:TPU:64 now
where the time goes in v1:
time: 122 us
  Pallas kernels  117 us (96%)
  other arithmetic  3.87 us (3%)
    pallas_call x1, Pallas kernels, shards(): pl.pallas_call(functools.partial(kernel, n_z), out_shape=(jax.ShapeDtypeS...  117 us
    convert_element_type x3, other arithmetic, shards(): return (y_tok.astype(F32), y_in[None].astype(F32), y_out[None].astype(F32))  3.87 us

profile of v1, /device:TPU:64, one launch (start us, length us, event | category | flops | bytes accessed | tf_op | source)
XLA Modules:
  0.0 121.7 jit_solution(3265621656972920149)
XLA Ops:
  0.6 117.1 %shard_map.112 = (bf16[128,2048]{1,0:T(8,128)(2,1)}, bf16[2,768,128]{2,1,0:T(8,128)(2,1)}, bf16[768,128]{1,0:T(8,128)(2,1)}) custom-call(s32[8,128]{1,0:T(8,128)} %bitcast.16, f32[8,128]{1,0:T(8,128)} %bitcast.17, bf16[128,2048]{1,0:T(8,128)(2,1)} %tok_ref.1, bf16[128,2048]{1,0:T(8,128)(2,1)} %tan_ref.1, bf16[128,2048]{1,0:T(8,128)(2,1)} %cot_ref.1, ...), custom_call_target="tpu_custom_call" | custom-call | tf_op jit(solution)/shard_map/pallas_call | solution.py:403
  117.8 0.0 copy-start
  117.8 2.2 %convert_element_type.15 = f32[128,2048]{1,0:T(8,128)} convert(bf16[128,2048]{1,0:T(8,128)(2,1)} %get-tuple-element.6) | non-fusion elementwise | flops 262144 | bytes 1572864 | tf_op jit(solution)/shard_map/convert_element_type | solution.py:465
  120.0 0.0 copy-done
  120.0 0.0 copy-start.1
  120.0 0.9 bitcast_convert_fusion
  120.9 0.0 copy-done.1
  120.9 0.8 bitcast_convert_fusion.1
Async XLA Ops:
  117.8 2.2 %copy-start = (bf16[2,768,128]{2,1,0:T(8,128)(2,1)S(1)}, bf16[2,768,128]{2,1,0:T(8,128)(2,1)}, u32[]{:S(2)}) copy-start(bf16[2,768,128]{2,1,0:T(8,128)(2,1)} %get-tuple-element.7) | copy-start | bytes 1179652
  120.0 1.0 copy-start.1

commit v2 on v1

v2 whole, which is shorter than its diff:
```python
import functools

import jax
import jax.numpy as jnp
from jax import lax
from jax.experimental import pallas as pl
from jax.experimental.pallas import tpu as pltpu
from jax.sharding import PartitionSpec as P

MESH = pl.DeviceIdType.MESH
F32 = jnp.float32
BF16 = jnp.bfloat16
SIDE = 4
NT = (((1,), (1,)), ((), ()))
NN = (((1,), (0,)), ((), ()))


def mm(a, b, dims=NN):
    return lax.dot_general(a, b, dims, preferred_element_type=F32)


def kernel(
    n_z, ids_ref, gates_ref, tok_ref, tan_ref, cot_ref, wi_ref, vi_ref, wo_ref, vo_ref,
    out_tok, out_in, out_out,
    W, stage, X, G, C, S, ST, H, acc, Pown, PDs, PDr, xs, xopp, xr, xropp, ys, yopp, yr, yropp, R, OUT, Zs, Zr, Zf,
    loc, wa_s, wa_r, st_s, st_r, sf_s, sf_r, wy_s, wy_r, wf_s, wf_r, xh_s, xh_r, xf_s, xf_r, zx_s, zx_r, zo_s, zo_r,
    g_s, g_r, gd, dd_s, dd_r, pd_s, pd_r,
    xo_s, xo_r, xp_s, xp_r, yo_s, yo_r, yp_s, yp_r, ra_s, ra_r, z1_s, z1_r, z2_s, z2_r,
):
    t = lax.axis_index("tensor")
    e = lax.axis_index("expert")
    p = lax.axis_index("dp")
    y, x = p // SIDE, p % SIDE
    color = lax.rem(t, 2)
    tok = tok_ref.shape[0]
    half = tok // 2
    quarter = tok // 4
    lanes = wi_ref.shape[-1]
    q = W.shape[1]
    width = W.shape[2]
    part = width // SIDE

    def at_x(d):
        return lax.rem(x + d, SIDE)

    def at_y(d):
        return lax.rem(y + d, SIDE)

    def dev_x(d):
        return (t, e, y * SIDE + at_x(d))

    def dev_y(d):
        return (t, e, at_y(d) * SIDE + x)

    def dev_z(d):
        return (lax.rem(t + d, n_z), e, p)

    partner = (t, 1 - e, p)
    pending = []

    def send(src, dst, ssem, rsem, dev):
        copy = pltpu.make_async_remote_copy(
            src_ref=src, dst_ref=dst, send_sem=ssem, recv_sem=rsem, device_id=dev, device_id_type=MESH
        )
        copy.start()
        pending.append(copy)

    def got(dst, ssem, rsem):
        pltpu.make_async_remote_copy(
            src_ref=dst, dst_ref=dst, send_sem=ssem, recv_sem=rsem, device_id=partner, device_id_type=MESH
        ).wait_recv()

    barrier = pltpu.get_barrier_semaphore()
    peers = [partner] + [dev_x(d) for d in (1, 2, 3)] + [dev_y(d) for d in (1, 3)] + [dev_z(d) for d in range(1, n_z)]
    for peer in peers:
        pl.semaphore_signal(barrier, inc=1, device_id=peer, device_id_type=MESH)

    def slab(yy, xx):
        return pl.ds(pl.multiple_of((yy * SIDE + xx) * lanes, lanes), lanes)

    def rows(k):
        return pl.ds(pl.multiple_of(k * q, q), q)

    mine = [
        pltpu.make_async_copy(wi_ref.at[:, rows(x), :], W.at[0:2, :, slab(y, x)], loc.at[3]),
        pltpu.make_async_copy(wo_ref.at[rows(x), :], W.at[2, :, slab(y, x)], loc.at[4]),
        pltpu.make_async_copy(vi_ref.at[:, rows(x), :], W.at[3:5, :, slab(y, x)], loc.at[5]),
        pltpu.make_async_copy(vo_ref.at[rows(x), :], W.at[5, :, slab(y, x)], loc.at[6]),
        pltpu.make_async_copy(tok_ref, X.at[0, x, e], loc.at[0]),
        pltpu.make_async_copy(tan_ref, X.at[1, x, e], loc.at[1]),
        pltpu.make_async_copy(cot_ref, X.at[2, x, e], loc.at[2]),
    ]
    for copy in mine:
        copy.start()
    ids, gates = ids_ref[...], gates_ref[...]
    for r in range(2):
        G[e, x, pl.ds(r, 1), :] = jnp.sum(jnp.where(ids == 2 * t + r, gates, 0.0), axis=0, keepdims=True)
    pl.semaphore_wait(barrier, len(peers))

    def thirds(buf, h):
        return (buf.at[h, 0:2], buf.at[h, 2])

    def in_w(h, at):
        return (W.at[3 * h : 3 * h + 2, :, at], W.at[3 * h + 2, :, at])

    def from_args(h, k):
        return ((wi_ref, vi_ref)[h].at[:, rows(k), :], (wo_ref, vo_ref)[h].at[rows(k), :])

    def quarter_to(h):
        for k, d in enumerate((1, 3)):
            for i, (src, to) in enumerate(zip(from_args(h, at_x(d)), in_w(h, slab(y, x)))):
                send(src, to, wa_s.at[k, 2 * h + i], wa_r.at[k, 2 * h + i], dev_x(d))

    quarter_to(0)
    for h in range(2):
        for i, (src, to) in enumerate(zip(from_args(h, at_x(2)), thirds(stage, h))):
            send(src, to, st_s.at[h, i], st_r.at[h, i], dev_x(1 + 2 * h))
    quarter_to(1)
    for k, d in enumerate((1, 3, 2)):
        send(G.at[e, x], G.at[e, x], g_s.at[k], g_r.at[k], dev_x(d))
    for copy in mine:
        copy.wait()

    def unit(yy, d, h):
        return W.at[3 * h : 3 * h + 3, :, slab(yy, at_x(SIDE - d))]

    order = (0, 1, 3, 2)

    def spread(d, h):
        k = order.index(d)
        for i in range(2):
            send(unit(y, d, h), unit(y, d, h), wy_s.at[i, k, h], wy_r.at[i, k, h], dev_y(1 + 2 * i))

    def onward(d):
        k = order.index(d)
        for h in range(2):
            at = unit(at_y(3 - 2 * h), d, h)
            got(at, wy_s.at[h, k, h], wy_r.at[h, k, h])
            send(at, at, wf_s.at[h, k], wf_r.at[h, k], dev_y(1 + 2 * h))

    def got_quarter(h):
        for k, d in enumerate((1, 3)):
            for i, to in enumerate(in_w(h, slab(y, at_x(SIDE - d)))):
                got(to, wa_s.at[k, 2 * h + i], wa_r.at[k, 2 * h + i])
            spread(d, h)

    spread(0, 0)
    spread(0, 1)
    send(X.at[:, x, e], X.at[:, x, e], dd_s.at[0, 0, 0], dd_r.at[0, 0, 0], partner)
    got_quarter(0)
    for h in range(2):
        for i, to in enumerate(thirds(stage, h)):
            got(to, st_s.at[h, i], st_r.at[h, i])
        for i, (src, to) in enumerate(zip(thirds(stage, h), in_w(h, slab(y, at_x(3 - 2 * h))))):
            send(src, to, sf_s.at[h, i], sf_r.at[h, i], dev_x(1 + 2 * h))

    def piece(a, own, h, core):
        first = (color if own else 1 - color) * half + h * quarter
        return X.at[:, a, core, pl.ds(pl.multiple_of(first, quarter), quarter), :]

    for k, h in ((0, 0), (1, 1), (0, 1), (1, 0)):
        part_of = piece(x, True, h, e)
        send(part_of, part_of, xh_s.at[k, h], xh_r.at[k, h], dev_x(1 + 2 * k))

    def to_core(rel, own, h):
        part_of = piece(at_x(SIDE - rel), own, h, e)
        k = 0 if own else 1
        send(part_of, part_of, dd_s.at[rel, k, h], dd_r.at[rel, k, h], partner)

    def eighth(a, own, h, s, core):
        first = (color if own else 1 - color) * half + h * quarter + s * (quarter // 2)
        return X.at[:, a, core, pl.ds(pl.multiple_of(first, quarter // 2), quarter // 2), :]

    def over_x(rel, h):
        a = at_x(SIDE - rel)
        plane = dev_z(1 if h == 0 else n_z - 1)
        if rel == 2:
            for s in range(2):
                at = eighth(a, True, h, s, e)
                got(at, xf_s.at[h, s], xf_r.at[h, s])
                send(at, at, zo_s.at[h, s], zo_r.at[h, s], plane)
        else:
            k = 0 if rel == 1 else 1
            at = piece(a, True, h, e)
            got(at, xh_s.at[k, h], xh_r.at[k, h])
            if h == k:
                for s in range(2):
                    sub = eighth(a, True, h, s, e)
                    send(sub, sub, xf_s.at[h, s], xf_r.at[h, s], dev_x(1 + 2 * k))
            send(at, at, zx_s.at[rel // 2, h], zx_r.at[rel // 2, h], plane)
        to_core(rel, True, h)

    def over_z(rel, h):
        a = at_x(SIDE - rel)
        if rel == 2:
            for s in range(2):
                got(eighth(a, False, h, s, e), zo_s.at[h, s], zo_r.at[h, s])
        else:
            got(piece(a, False, h, e), zx_s.at[rel // 2, h], zx_r.at[rel // 2, h])
        to_core(rel, False, h)

    got_quarter(1)
    for h in range(2):
        for i, to in enumerate(in_w(h, slab(y, at_x(2)))):
            got(to, sf_s.at[h, i], sf_r.at[h, i])
        spread(2, h)
    onward(0)
    onward(1)
    onward(3)
    over_x(1, 0)
    over_x(3, 1)
    onward(2)
    for k, d in enumerate((1, 3, 2)):
        got(G.at[e, at_x(SIDE - d)], g_s.at[k], g_r.at[k])
    send(G.at[e], G.at[e], gd.at[0], gd.at[1], partner)
    over_x(1, 1)
    over_x(3, 0)
    over_z(1, 0)
    over_z(3, 1)
    over_x(2, 0)
    over_x(2, 1)
    over_z(3, 0)
    over_z(1, 1)
    for k, d in enumerate(order):
        for h in range(2):
            got(unit(at_y(3 - 2 * h), d, 1 - h), wy_s.at[h, k, 1 - h], wy_r.at[h, k, 1 - h])
            got(unit(at_y(2), d, h), wf_s.at[h, k], wf_r.at[h, k])
    got(G.at[1 - e], gd.at[0], gd.at[1])

    n_acc = acc.shape[1]
    cut = n_acc // 2
    step = 32

    def tokens_of(a):
        return pl.ds(pl.multiple_of(a * 2 * tok, 2 * tok), 2 * tok)

    def forward(rel):
        a = at_x(SIDE - rel)
        if rel == 0:
            got(X.at[:, x, 1 - e], dd_s.at[0, 0, 0], dd_r.at[0, 0, 0])
        else:
            for k in range(2):
                for h in range(2):
                    got(piece(a, k == 0, h, 1 - e), dd_s.at[rel, k, h], dd_r.at[rel, k, h])

        def both(i):
            return X[i, a].reshape(2 * tok, width)

        C[0 : 2 * q, :] = mm(W[0:2].reshape(2 * q, width), both(0), NT)
        C[2 * q : 4 * q, :] = mm(W[3:5].reshape(2 * q, width), both(0), NT)
        C[4 * q : 6 * q, :] = mm(W[0:2].reshape(2 * q, width), both(1), NT)
        C[6 * q : 7 * q, :] = mm(W[2], both(2), NT)
        C[7 * q : 8 * q, :] = mm(W[5], both(2), NT)
        gate = jnp.concatenate([G[0, a, pl.ds(e, 1), :], G[1, a, pl.ds(e, 1), :]], axis=1)
        cols = tokens_of(a)

        def rows_of(i, carry):
            at = pl.multiple_of(i * step, step)

            def c(k):
                return C[pl.ds(k * q + at, step), :]

            pre, up = c(0), c(1)
            pre_dot, up_dot = c(4) + c(2), c(5) + c(3)
            g, g_dot = c(6) * gate, c(7) * gate
            sigma = jax.nn.sigmoid(pre)
            rest = 1.0 - sigma
            s0 = pre * sigma
            s1 = sigma * (1.0 + pre * rest)
            s2 = sigma * rest * (2.0 + pre * (1.0 - 2.0 * sigma))
            S[pl.ds(at, step), cols] = (
                g_dot * up * s1 + g * up_dot * s1 + g * up * s2 * pre_dot
            ).astype(BF16)
            S[pl.ds(q + at, step), cols] = (g_dot * s0 + g * s1 * pre_dot).astype(BF16)
            S[pl.ds(2 * q + at, step), cols] = (g * up * s1).astype(BF16)
            S[pl.ds(3 * q + at, step), cols] = (g * s0).astype(BF16)
            H[pl.ds(at, step), cols] = ((s1 * pre_dot * up + s0 * up_dot) * gate).astype(BF16)
            return carry

        lax.fori_loop(0, q // step, rows_of, 0)
        ST[rel] = S[:, cols].T

    def tokens_back(n):
        cols = slice(n * part, (n + 1) * part)
        for rel in (2, 1, 3, 0):
            value = mm(ST[rel, :, 0 : 2 * q], W[0:2, :, cols].reshape(2 * q, part))
            value += mm(ST[rel, :, 2 * q : 4 * q], W[3:5, :, cols].reshape(2 * q, part))
            for core in range(2):

                @pl.when(e == core)
                def _():
                    Pown[rel, n] = value[core * tok : (core + 1) * tok]
                    PDs[rel, n] = value[(1 - core) * tok : (2 - core) * tok].astype(BF16)

            send(PDs.at[rel, n], PDr.at[rel, n], pd_s.at[rel, n], pd_r.at[rel, n], partner)

    def weights_back(n):
        cols = pl.ds(pl.multiple_of(n * part, part), part)

        def every(i):
            return X[i, :, :, :, cols].reshape(SIDE * 2 * tok, part)

        acc[n, 0 : 2 * q, :] = mm(S[2 * q : 4 * q, :], every(1)) + mm(S[0 : 2 * q, :], every(0))
        acc[n, 2 * q : 3 * q, :] = mm(H[...], every(2))

    def summed(rel, n, h):
        at = pl.ds(h * half, half)
        return Pown[rel, n, at, :] + PDr[rel, n, at, :].astype(F32)

    def acc_half(k, h):
        return acc[k, h * cut : (h + 1) * cut, :]

    def x_first(n):
        for rel in (2, 1, 3):
            got(PDr.at[rel, n], pd_s.at[rel, n], pd_r.at[rel, n])
            if rel == 2:
                for h in range(2):
                    xopp[n, h] = summed(2, n, h).astype(BF16)
                    send(xopp.at[n, h], xropp.at[n, h], xo_s.at[n, h], xo_r.at[n, h], dev_x(1 + 2 * h))
            else:
                k, h = (1, 0) if rel == 1 else (0, 1)
                xs[n, k, h] = summed(rel, n, h).astype(BF16)
                send(xs.at[n, k, h], xr.at[n, k, h], xp_s.at[n, k, h], xp_r.at[n, k, h], dev_x(1 + 2 * k))

    def x_second(n):
        for k in range(2):
            got(xropp.at[n, k], xo_s.at[n, k], xo_r.at[n, k])
            xs[n, k, k] = (summed(3 - 2 * k, n, k) + xropp[n, k].astype(F32)).astype(BF16)
            send(xs.at[n, k, k], xr.at[n, k, k], xp_s.at[n, k, k], xp_r.at[n, k, k], dev_x(1 + 2 * k))

    piece_z = tok // n_z

    def z_scatter(n):
        got(PDr.at[0, n], pd_s.at[0, n], pd_r.at[0, n])
        for h in range(2):
            for k in range(2):
                got(xr.at[n, k, h], xp_s.at[n, k, h], xp_r.at[n, k, h])
            total = summed(0, n, h) + xr[n, 0, h].astype(F32) + xr[n, 1, h].astype(F32)
            at = pl.ds(h * (n_z // 2), n_z // 2)
            Zs[n, at] = total.reshape(n_z // 2, piece_z, part).astype(BF16)
        Zr[n, t] = Zs[n, t]
        for d in range(1, n_z):
            send(Zs.at[n, lax.rem(t + d, n_z)], Zr.at[n, t], z1_s.at[n, d - 1], z1_r.at[n, d - 1], dev_z(d))

    def z_gather(n):
        for d in range(1, n_z):
            got(Zr.at[n, lax.rem(t + n_z - d, n_z)], z1_s.at[n, d - 1], z1_r.at[n, d - 1])
        done = Zr[n, 0].astype(F32)
        for k in range(1, n_z):
            done += Zr[n, k].astype(F32)
        Zf[n, t] = done.astype(BF16)
        for d in range(1, n_z):
            send(Zf.at[n, t], Zf.at[n, t], z2_s.at[n, d - 1], z2_r.at[n, d - 1], dev_z(d))

    def y_first():
        weights_back(at_y(2))
        for h in range(2):
            yopp[h] = acc_half(at_y(2), h).astype(BF16)
            send(yopp.at[h], yropp.at[h], yo_s.at[h], yo_r.at[h], dev_y(1 + 2 * h))

    def y_next(k):
        h = 1 - k
        weights_back(at_y(1 + 2 * k))
        ys[k, h] = acc_half(at_y(1 + 2 * k), h).astype(BF16)
        send(ys.at[k, h], yr.at[k, h], yp_s.at[k, h], yp_r.at[k, h], dev_y(1 + 2 * k))

    def y_second():
        for k in range(2):
            got(yropp.at[k], yo_s.at[k], yo_r.at[k])
            ys[k, k] = (acc_half(at_y(1 + 2 * k), k) + yropp[k].astype(F32)).astype(BF16)
            send(ys.at[k, k], yr.at[k, k], yp_s.at[k, k], yp_r.at[k, k], dev_y(1 + 2 * k))

    def x_slices():
        for h in range(2):
            for k in range(2):
                got(yr.at[k, h], yp_s.at[k, h], yp_r.at[k, h])
            value = acc_half(y, h) + yr[0, h].astype(F32) + yr[1, h].astype(F32)
            value = value.astype(BF16)
            for k in range(SIDE):
                R[h, k] = value[:, k * lanes : (k + 1) * lanes]
            OUT[x, h] = R[h, x]
            for k, d in enumerate((1, 3, 2)):
                send(R.at[h, at_x(d)], OUT.at[x, h], ra_s.at[h, k], ra_r.at[h, k], dev_x(d))

    forward(0)
    forward(1)
    over_z(2, 0)
    over_z(2, 1)
    forward(3)
    forward(2)
    tokens_back(0)
    x_first(0)
    y_first()
    tokens_back(1)
    x_first(1)
    x_second(0)
    tokens_back(2)
    x_first(2)
    y_next(0)
    x_second(1)
    tokens_back(3)
    x_first(3)
    y_next(1)
    x_second(2)
    z_scatter(0)
    weights_back(y)
    x_second(3)
    z_scatter(1)
    y_second()
    z_scatter(2)
    z_gather(0)
    z_scatter(3)
    z_gather(1)
    x_slices()
    z_gather(2)
    z_gather(3)

    for h in range(2):
        for k, d in enumerate((1, 3, 2)):
            got(OUT.at[at_x(SIDE - d), h], ra_s.at[h, k], ra_r.at[h, k])
    for k in range(SIDE):
        at = slice(k * q, (k + 1) * q)
        whole = OUT[k].reshape(n_acc, lanes)
        for i in range(2):
            out_in[i, at, :] = whole[i * q : (i + 1) * q]
        out_out[at, :] = whole[2 * q : 3 * q]

    for n in range(SIDE):
        for d in range(1, n_z):
            got(Zf.at[n, lax.rem(t + n_z - d, n_z)], z2_s.at[n, d - 1], z2_r.at[n, d - 1])
        out_tok[:, n * part : (n + 1) * part] = Zf[n].reshape(tok, part)
    for copy in pending:
        copy.wait_send()


def shards(n_z, tokens, tangent, cotangent, expert_ids, gates, w_in, v_in, w_out, v_out):
    tok = tokens.shape[0]
    ff, lanes = w_in.shape[2:]
    width = tokens.shape[1]
    q = ff // SIDE
    half = tok // 2
    part = width // SIDE
    cut = 3 * q // 2
    dma = pltpu.SemaphoreType.DMA
    vmem = pl.BlockSpec(memory_space=pltpu.VMEM)
    hbm = pl.BlockSpec(memory_space=pltpu.HBM)
    y_tok, y_in, y_out = pl.pallas_call(
        functools.partial(kernel, n_z),
        out_shape=(
            jax.ShapeDtypeStruct((tok, width), BF16),
            jax.ShapeDtypeStruct((2, ff, lanes), BF16),
            jax.ShapeDtypeStruct((ff, lanes), BF16),
        ),
        in_specs=[vmem, vmem] + [hbm] * 7,
        out_specs=(vmem, vmem, vmem),
        scratch_shapes=[
            pltpu.VMEM((6, q, width), BF16),
            pltpu.VMEM((2, 3, q, lanes), BF16),
            pltpu.VMEM((3, SIDE, 2, tok, width), BF16),
            pltpu.VMEM((2, SIDE, 8, tok), F32),
            pltpu.VMEM((8 * q, 2 * tok), F32),
            pltpu.VMEM((4 * q, SIDE * 2 * tok), BF16),
            pltpu.VMEM((4, 2 * tok, 4 * q), BF16),
            pltpu.VMEM((q, SIDE * 2 * tok), BF16),
            pltpu.VMEM((SIDE, 3 * q, part), F32),
            pltpu.VMEM((4, SIDE, tok, part), F32),
            pltpu.VMEM((4, SIDE, tok, part), BF16),
            pltpu.VMEM((4, SIDE, tok, part), BF16),
            pltpu.VMEM((SIDE, 2, 2, half, part), BF16),
            pltpu.VMEM((SIDE, 2, half, part), BF16),
            pltpu.VMEM((SIDE, 2, 2, half, part), BF16),
            pltpu.VMEM((SIDE, 2, half, part), BF16),
            pltpu.VMEM((2, 2, cut, part), BF16),
            pltpu.VMEM((2, cut, part), BF16),
            pltpu.VMEM((2, 2, cut, part), BF16),
            pltpu.VMEM((2, cut, part), BF16),
            pltpu.VMEM((2, SIDE, cut, lanes), BF16),
            pltpu.VMEM((SIDE, 2, cut, lanes), BF16),
            pltpu.VMEM((SIDE, n_z, tok // n_z, part), BF16),
            pltpu.VMEM((SIDE, n_z, tok // n_z, part), BF16),
            pltpu.VMEM((SIDE, n_z, tok // n_z, part), BF16),
            dma((7,)),
            dma((2, 4)), dma((2, 4)),
            dma((2, 2)), dma((2, 2)),
            dma((2, 2)), dma((2, 2)),
            dma((2, 4, 2)), dma((2, 4, 2)),
            dma((2, 4)), dma((2, 4)),
            dma((2, 2)), dma((2, 2)),
            dma((2, 2)), dma((2, 2)),
            dma((2, 2)), dma((2, 2)),
            dma((2, 2)), dma((2, 2)),
            dma((3,)), dma((3,)),
            dma((2,)),
            dma((4, 2, 2)), dma((4, 2, 2)),
            dma((4, 4)), dma((4, 4)),
            dma((4, 2)), dma((4, 2)),
            dma((4, 2, 2)), dma((4, 2, 2)),
            dma((2,)), dma((2,)),
            dma((2, 2)), dma((2, 2)),
            dma((2, 3)), dma((2, 3)),
            dma((4, n_z - 1)), dma((4, n_z - 1)),
            dma((4, n_z - 1)), dma((4, n_z - 1)),
        ],
        compiler_params=pltpu.CompilerParams(
            collective_id=0, has_side_effects=True, vmem_limit_bytes=62 * 1024 * 1024
        ),
    )(
        expert_ids.T, gates.T, tokens, tangent, cotangent, w_in[0], v_in[0], w_out[0], v_out[0]
    )
    return y_tok.astype(F32), y_in[None].astype(F32), y_out[None].astype(F32)


def solution(mesh):
    rows = P(("expert", "dp"), None)
    w_spec = P(("tensor", "expert"), None, None, "dp")
    o_spec = P(("tensor", "expert"), None, "dp")
    return jax.shard_map(
        functools.partial(shards, mesh.shape["tensor"]),
        mesh=mesh,
        in_specs=(rows,) * 5 + (w_spec, w_spec, o_spec, o_spec),
        out_specs=(rows, w_spec, o_spec),
        check_vma=False,
    )
```

time: 122 us -> 116 us (0.951)
  the two profiles are of different devices: /device:TPU:64 before, /device:TPU:24 now
where the time goes in v2:
time: 116 us; the launch traced here: 115 us
  Pallas kernels  111 us (96%)
  other arithmetic  3.87 us (3%)
    pallas_call x1, Pallas kernels, shards(): pl.pallas_call(functools.partial(kernel, n_z), out_shape=(jax.ShapeDtypeS...  111 us
    convert_element_type x3, other arithmetic, shards(): return (y_tok.astype(F32), y_in[None].astype(F32), y_out[None].astype(F32))  3.87 us

profile of v2, /device:TPU:24, one launch (start us, length us, event | category | flops | bytes accessed | tf_op | source)
XLA Modules:
  0.0 115.4 jit_solution(14781642987479879937)
XLA Ops:
  0.6 110.8 %shard_map.112 = (bf16[128,2048]{1,0:T(8,128)(2,1)}, bf16[2,768,128]{2,1,0:T(8,128)(2,1)}, bf16[768,128]{1,0:T(8,128)(2,1)}) custom-call(s32[8,128]{1,0:T(8,128)} %bitcast.16, f32[8,128]{1,0:T(8,128)} %bitcast.17, bf16[128,2048]{1,0:T(8,128)(2,1)} %tok_ref.1, bf16[128,2048]{1,0:T(8,128)(2,1)} %tan_ref.1, bf16[128,2048]{1,0:T(8,128)(2,1)} %cot_ref.1, ...), custom_call_target="tpu_custom_call" | custom-call | tf_op jit(solution)/shard_map/pallas_call | solution.py:447
  111.5 0.0 copy-start
  111.5 2.2 %convert_element_type.15 = f32[128,2048]{1,0:T(8,128)} convert(bf16[128,2048]{1,0:T(8,128)(2,1)} %get-tuple-element.6) | non-fusion elementwise | flops 262144 | bytes 1572864 | tf_op jit(solution)/shard_map/convert_element_type | solution.py:510
  113.6 0.0 copy-done
  113.6 0.0 copy-start.1
  113.6 0.9 bitcast_convert_fusion
  114.6 0.0 copy-done.1
  114.6 0.8 bitcast_convert_fusion.1
Async XLA Ops:
  111.5 2.2 %copy-start = (bf16[2,768,128]{2,1,0:T(8,128)(2,1)S(1)}, bf16[2,768,128]{2,1,0:T(8,128)(2,1)}, u32[]{:S(2)}) copy-start(bf16[2,768,128]{2,1,0:T(8,128)(2,1)} %get-tuple-element.7) | copy-start | bytes 1179652
  113.6 1.0 copy-start.1

commit v3 on v2

v3 whole, which is shorter than its diff:
```python
import functools

import jax
import jax.numpy as jnp
from jax import lax
from jax.experimental import pallas as pl
from jax.experimental.pallas import tpu as pltpu
from jax.sharding import PartitionSpec as P

MESH = pl.DeviceIdType.MESH
F32 = jnp.float32
BF16 = jnp.bfloat16
SIDE = 4
NT = (((1,), (1,)), ((), ()))
NN = (((1,), (0,)), ((), ()))


def mm(a, b, dims=NN):
    return lax.dot_general(a, b, dims, preferred_element_type=F32)


def kernel(
    n_z, ids_ref, gates_ref, tok_ref, tan_ref, cot_ref, wi_ref, vi_ref, wo_ref, vo_ref,
    out_tok, out_in, out_out,
    W, Wsrc, stage, X, G, C, S, ST, H, acc, Pown, PDs, PDr, xs, xopp, xr, xropp, ys, yopp, yr, yropp, R, OUT, Zt, Zs, Z3, Zm, Zr, Zf,
    loc, snd, wa_r, st_r, sf_r, wy_r, wrest, xh_r, xf_r, zx_r, g_r, dd_r, pd_r, xo_r, xp_r, yo_r, yp_r, ra_r,
    z1_r, z4_r, z2_r, zd_r,
):
    t = lax.axis_index("tensor")
    e = lax.axis_index("expert")
    p = lax.axis_index("dp")
    y, x = p // SIDE, p % SIDE
    color = lax.rem(t, 2)
    tok = tok_ref.shape[0]
    half = tok // 2
    quarter = tok // 4
    lanes = wi_ref.shape[-1]
    q = W.shape[2]
    width = tok_ref.shape[1]
    part = width // SIDE

    def at_x(d):
        return lax.rem(x + d, SIDE)

    def at_y(d):
        return lax.rem(y + d, SIDE)

    def dev_x(d):
        return (t, e, y * SIDE + at_x(d))

    def dev_y(d):
        return (t, e, at_y(d) * SIDE + x)

    def dev_z(d):
        return (lax.rem(t + d, n_z), e, p)

    partner = (t, 1 - e, p)
    s_w, s_x, s_pd, s_xo, s_xs, s_yo, s_ys, s_r, s_z, s_g, s_gd = (snd.at[i] for i in range(11))

    def send(src, dst, ssem, rsem, dev):
        pltpu.make_async_remote_copy(
            src_ref=src, dst_ref=dst, send_sem=ssem, recv_sem=rsem, device_id=dev, device_id_type=MESH
        ).start()

    def got(ref, rsem):
        pltpu.make_async_remote_copy(
            src_ref=ref, dst_ref=ref, send_sem=s_w, recv_sem=rsem, device_id=partner, device_id_type=MESH
        ).wait_recv()

    def sent(ref, ssem):
        pltpu.make_async_remote_copy(
            src_ref=ref, dst_ref=ref, send_sem=ssem, recv_sem=ssem, device_id=partner, device_id_type=MESH
        ).wait_send()

    barrier = pltpu.get_barrier_semaphore()
    peers = [partner] + [dev_x(d) for d in (1, 2, 3)] + [dev_y(d) for d in (1, 3)] + [dev_z(d) for d in (1, 2, n_z - 2, n_z - 1)]
    for peer in peers:
        pl.semaphore_signal(barrier, inc=1, device_id=peer, device_id_type=MESH)

    def rows(k):
        return pl.ds(pl.multiple_of(k * q, q), q)

    for src, dst, i in (
        (wi_ref, Wsrc.at[0:2], 0),
        (wo_ref, Wsrc.at[2], 0),
        (vi_ref, Wsrc.at[3:5], 0),
        (vo_ref, Wsrc.at[5], 0),
        (wi_ref.at[:, rows(x), :], W.at[p, 0:2], 1),
        (wo_ref.at[rows(x), :], W.at[p, 2], 1),
        (vi_ref.at[:, rows(x), :], W.at[p, 3:5], 1),
        (vo_ref.at[rows(x), :], W.at[p, 5], 1),
        (tok_ref, X.at[0, x, e], 2),
        (tan_ref, X.at[1, x, e], 2),
        (cot_ref, X.at[2, x, e], 2),
    ):
        pltpu.make_async_copy(src, dst, loc.at[i]).start()
    ids, gates = ids_ref[...], gates_ref[...]
    for r in range(2):
        G[e, x, pl.ds(r, 1), :] = jnp.sum(jnp.where(ids == 2 * t + r, gates, 0.0), axis=0, keepdims=True)
    pl.semaphore_wait(barrier, len(peers))

    got(Wsrc, loc.at[0])

    def quarter_of(h, k):
        return Wsrc.at[3 * h : 3 * h + 3, rows(k), :]

    def unit(yy, d, h):
        return W.at[yy * SIDE + at_x(SIDE - d), 3 * h : 3 * h + 3]

    def quarter_to(h):
        for k, d in enumerate((1, 3)):
            send(quarter_of(h, at_x(d)), unit(y, 0, h), s_w, wa_r.at[k, h], dev_x(d))

    quarter_to(0)
    for h in range(2):
        send(quarter_of(h, at_x(2)), stage.at[h], s_w, st_r.at[h], dev_x(1 + 2 * h))
    quarter_to(1)
    for d in (1, 3, 2):
        send(G.at[e, x], G.at[e, x], s_g, g_r.at[0], dev_x(d))
    got(W.at[p], loc.at[1])

    order = (0, 1, 3, 2)

    def spread(d, h):
        k = order.index(d)
        for i in range(2):
            sem = wy_r.at[i, k] if i == h else wrest.at[0]
            send(unit(y, d, h), unit(y, d, h), s_w, sem, dev_y(1 + 2 * i))

    def onward(d):
        k = order.index(d)
        for h in range(2):
            at = unit(at_y(3 - 2 * h), d, h)
            got(at, wy_r.at[h, k])
            send(at, at, s_w, wrest.at[0], dev_y(1 + 2 * h))

    def got_quarter(h):
        for k, d in enumerate((1, 3)):
            got(unit(y, d, h), wa_r.at[k, h])
            spread(d, h)

    spread(0, 0)
    spread(0, 1)
    got(X.at[:, x, e], loc.at[2])
    send(X.at[:, x, e], X.at[:, x, e], s_x, dd_r.at[0], partner)
    got_quarter(0)
    for h in range(2):
        got(stage.at[h], st_r.at[h])
        send(stage.at[h], unit(y, 1 + 2 * h, h), s_w, sf_r.at[h], dev_x(1 + 2 * h))

    def piece(a, own, h, i):
        eighth = quarter // 2
        first = (color if own else 1 - color) * half + h * quarter + i * eighth
        return X.at[:, a, e, pl.ds(pl.multiple_of(first, eighth), eighth), :]

    for k, h in ((0, 0), (1, 1), (0, 1), (1, 0)):
        for i in range(2):
            at = piece(x, True, h, i)
            send(at, at, s_x, xh_r.at[k, h, i], dev_x(1 + 2 * k))

    def over_x(rel, h, i):
        at = piece(at_x(SIDE - rel), True, h, i)
        if rel == 2:
            got(at, xf_r.at[h, i])
        else:
            k = rel // 2
            got(at, xh_r.at[k, h, i])
            if h == k:
                send(at, at, s_x, xf_r.at[h, i], dev_x(1 + 2 * k))
        send(at, at, s_x, zx_r.at[rel - 1, h, i], dev_z(1 if h == 0 else n_z - 1))
        send(at, at, s_x, dd_r.at[rel], partner)

    def over_z(rel, h, i):
        at = piece(at_x(SIDE - rel), False, h, i)
        got(at, zx_r.at[rel - 1, h, i])
        send(at, at, s_x, dd_r.at[rel], partner)

    got_quarter(1)
    for h in range(2):
        got(unit(y, 2, h), sf_r.at[h])
        spread(2, h)
    onward(0)
    onward(1)
    over_x(1, 0, 0)
    over_x(3, 1, 0)
    got(G.at[e, 0:3], g_r.at[0])
    send(G.at[e], G.at[e], s_gd, g_r.at[1], partner)
    onward(3)
    over_x(1, 0, 1)
    over_x(3, 1, 1)
    over_z(1, 0, 0)
    over_z(3, 1, 0)
    onward(2)
    over_x(1, 1, 0)
    over_x(3, 0, 0)
    over_z(1, 0, 1)
    over_z(3, 1, 1)
    over_x(1, 1, 1)
    over_x(3, 0, 1)
    over_z(3, 0, 0)
    over_z(1, 1, 0)
    over_x(2, 0, 0)
    over_x(2, 1, 0)
    over_z(3, 0, 1)
    over_z(1, 1, 1)
    over_x(2, 0, 1)
    over_x(2, 1, 1)
    got(W.at[0:8], wrest.at[0])
    got(G.at[1 - e], g_r.at[1])

    n_acc = acc.shape[1]
    cut = n_acc // 2
    step = 32

    def tokens_of(a):
        return pl.ds(pl.multiple_of(a * 2 * tok, 2 * tok), 2 * tok)

    def weights(lo, hi, slabs=range(SIDE * SIDE)):
        return jnp.concatenate([W[k, lo:hi].reshape((hi - lo) * q, lanes) for k in slabs], axis=1)

    def turn(rel):
        ST[rel] = S[:, tokens_of(at_x(SIDE - rel))].T

    def forward(rel, before=None):
        a = at_x(SIDE - rel)
        got(X.at[:, a, 1 - e], dd_r.at[rel])
        if before is not None:
            turn(before)

        def both(i):
            return X[i, a].reshape(2 * tok, width)

        C[0 : 2 * q, :] = mm(weights(0, 2), both(0), NT)
        C[2 * q : 4 * q, :] = mm(weights(3, 5), both(0), NT)
        C[4 * q : 6 * q, :] = mm(weights(0, 2), both(1), NT)
        C[6 * q : 7 * q, :] = mm(weights(2, 3), both(2), NT)
        C[7 * q : 8 * q, :] = mm(weights(5, 6), both(2), NT)
        gate = jnp.concatenate([G[0, a, pl.ds(e, 1), :], G[1, a, pl.ds(e, 1), :]], axis=1)
        cols = tokens_of(a)

        def rows_of(i, carry):
            at = pl.multiple_of(i * step, step)

            def c(k):
                return C[pl.ds(k * q + at, step), :]

            pre, up = c(0), c(1)
            pre_dot, up_dot = c(4) + c(2), c(5) + c(3)
            g, g_dot = c(6) * gate, c(7) * gate
            sigma = jax.nn.sigmoid(pre)
            rest = 1.0 - sigma
            s0 = pre * sigma
            s1 = sigma * (1.0 + pre * rest)
            s2 = sigma * rest * (2.0 + pre * (1.0 - 2.0 * sigma))
            S[pl.ds(at, step), cols] = (
                g_dot * up * s1 + g * up_dot * s1 + g * up * s2 * pre_dot
            ).astype(BF16)
            S[pl.ds(q + at, step), cols] = (g_dot * s0 + g * s1 * pre_dot).astype(BF16)
            S[pl.ds(2 * q + at, step), cols] = (g * up * s1).astype(BF16)
            S[pl.ds(3 * q + at, step), cols] = (g * s0).astype(BF16)
            H[pl.ds(at, step), cols] = ((s1 * pre_dot * up + s0 * up_dot) * gate).astype(BF16)
            return carry

        lax.fori_loop(0, q // step, rows_of, 0)

    def tokens_back(n, rels):
        slabs = range(SIDE * n, SIDE * n + SIDE)
        for rel in rels:
            left = jnp.concatenate(
                [ST[rel, pl.ds(pl.multiple_of(k * tok, tok), tok), :] for k in (e, 1 - e)], axis=0
            )
            value = mm(left[:, 0 : 2 * q], weights(0, 2, slabs)) + mm(left[:, 2 * q : 4 * q], weights(3, 5, slabs))
            Pown[rel, n] = value[0:tok]
            PDs[rel, n] = value[tok : 2 * tok].astype(BF16)
            send(PDs.at[rel, n], PDr.at[rel, n], s_pd, pd_r.at[rel, n], partner)

    def weights_back(n):
        cols = pl.ds(pl.multiple_of(n * part, part), part)

        def every(i):
            return X[i, :, :, :, cols].reshape(SIDE * 2 * tok, part)

        acc[n, 0 : 2 * q, :] = mm(S[2 * q : 4 * q, :], every(1)) + mm(S[0 : 2 * q, :], every(0))
        acc[n, 2 * q : 3 * q, :] = mm(H[...], every(2))

    def summed(rel, n, h):
        at = pl.ds(h * half, half)
        return Pown[rel, n, at, :] + PDr[rel, n, at, :].astype(F32)

    def acc_half(k, h):
        return acc[k, h * cut : (h + 1) * cut, :]

    def x_first(n):
        for rel in (2, 1, 3):
            got(PDr.at[rel, n], pd_r.at[rel, n])
            if rel == 2:
                for h in range(2):
                    xopp[n, h] = summed(2, n, h).astype(BF16)
                    send(xopp.at[n, h], xropp.at[n, h], s_xo, xo_r.at[n, h], dev_x(1 + 2 * h))
            else:
                k, h = (1, 0) if rel == 1 else (0, 1)
                xs[n, k, h] = summed(rel, n, h).astype(BF16)
                send(xs.at[n, k, h], xr.at[n, k, h], s_xs, xp_r.at[n], dev_x(1 + 2 * k))

    def x_second(n):
        for k in range(2):
            got(xropp.at[n, k], xo_r.at[n, k])
            xs[n, k, k] = (summed(3 - 2 * k, n, k) + xropp[n, k].astype(F32)).astype(BF16)
            send(xs.at[n, k, k], xr.at[n, k, k], s_xs, xp_r.at[n], dev_x(1 + 2 * k))

    piece_z = tok // n_z

    def at_z(d):
        return lax.rem(t + d + n_z, n_z)

    mid = part // 2

    def lane_half(h):
        return slice(h * mid, (h + 1) * mid)

    def z_scatter(n):
        got(PDr.at[0, n], pd_r.at[0, n])
        got(xr.at[n], xp_r.at[n])
        for h in range(2):
            total = summed(0, n, h) + xr[n, 0, h].astype(F32) + xr[n, 1, h].astype(F32)
            total = total.reshape(n_z // 2, piece_z, part)
            at = pl.ds(h * (n_z // 2), n_z // 2)
            Zt[n, at] = total
            Zs[n, at] = total.astype(BF16)
        for k in range(2):
            far = at_z(3 - 6 * k)
            send(Zs.at[n, far], Z3.at[n, k, :, 0:part], s_z, z1_r.at[n, k], dev_z(2 + (n_z - 4) * k))
            src = Zs.at[n, at_z(4), :, lane_half(k)]
            send(src, Z3.at[n, k, :, part:], s_z, z1_r.at[n, k], dev_z(2 + (n_z - 4) * k))

    def z_middle(n):
        for k in range(2):
            sign = 1 - 2 * k
            got(Z3.at[n, k], z1_r.at[n, k])
            Zm[n, 0, k] = (Zt[n, at_z(sign)] + Z3[n, k, :, 0:part].astype(F32)).astype(BF16)
            send(Zm.at[n, 0, k], Zr.at[n, 0, k], s_z, z4_r.at[n], dev_z((sign + n_z) % n_z))
            here, there = lane_half(k), lane_half(1 - k)
            next_but_one = at_z(2 * sign)
            Zm[n, 1, k, :, here] = (Zt[n, next_but_one, :, here] + Z3[n, k, :, part:].astype(F32)).astype(BF16)
            Zm[n, 1, k, :, there] = Zt[n, next_but_one, :, there].astype(BF16)
            send(Zm.at[n, 1, k], Zr.at[n, 1, k], s_z, z4_r.at[n], dev_z((2 * sign + n_z) % n_z))

    def z_gather(n):
        done = Zt[n, t]
        got(Zr.at[n], z4_r.at[n])
        for i in range(2):
            for k in range(2):
                done += Zr[n, i, k].astype(F32)
        Zf[n, t] = done.astype(BF16)
        for i in (1, 0):
            for k in range(2):
                d = (i + 1) * (1 - 2 * k)
                sem = (zd_r if i == 0 else z2_r).at[n]
                send(Zf.at[n, t], Zf.at[n, t], s_z, sem, dev_z((d + n_z) % n_z))

    def z_relay(n):
        got(Zf.at[n, 0:2], z2_r.at[n])
        for k in range(2):
            sign = 1 - 2 * k
            src = at_z(-2 * sign)
            send(Zf.at[n, src], Zf.at[n, src], s_z, zd_r.at[n], dev_z((sign + n_z) % n_z))
            at = Zf.at[n, src, :, lane_half(k)]
            send(at, at, s_z, zd_r.at[n], dev_z((2 * sign + n_z) % n_z))

    def z_done(n):
        got(Zf.at[n, 0:5], zd_r.at[n])
        pltpu.make_async_copy(Zf.at[n], out_tok.at[:, :, n * part : (n + 1) * part], loc.at[3]).start()

    def y_first():
        weights_back(at_y(2))
        for h in range(2):
            yopp[h] = acc_half(at_y(2), h).astype(BF16)
            send(yopp.at[h], yropp.at[h], s_yo, yo_r.at[h], dev_y(1 + 2 * h))

    def y_next(k):
        h = 1 - k
        weights_back(at_y(1 + 2 * k))
        ys[k, h] = acc_half(at_y(1 + 2 * k), h).astype(BF16)
        send(ys.at[k, h], yr.at[k, h], s_ys, yp_r.at[k, h], dev_y(1 + 2 * k))

    def y_second():
        for k in range(2):
            got(yropp.at[k], yo_r.at[k])
            ys[k, k] = (acc_half(at_y(1 + 2 * k), k) + yropp[k].astype(F32)).astype(BF16)
            send(ys.at[k, k], yr.at[k, k], s_ys, yp_r.at[k, k], dev_y(1 + 2 * k))

    def x_slices():
        for h in range(2):
            for k in range(2):
                got(yr.at[k, h], yp_r.at[k, h])
            value = acc_half(y, h) + yr[0, h].astype(F32) + yr[1, h].astype(F32)
            value = value.astype(BF16)
            for k in range(SIDE):
                R[h, k] = value[:, k * lanes : (k + 1) * lanes]
            OUT[x, h] = R[h, x]
            for d in (1, 3, 2):
                send(R.at[h, at_x(d)], OUT.at[x, h], s_r, ra_r.at[0], dev_x(d))

    def weights_out():
        got(OUT.at[0:3], ra_r.at[0])
        for k in range(SIDE):
            first, rest = k * q, n_acc - cut - q
            for src, dst in (
                (OUT.at[k, 0, 0:q], out_in.at[0, first : first + q]),
                (OUT.at[k, 0, q:cut], out_in.at[1, first : first + cut - q]),
                (OUT.at[k, 1, 0:rest], out_in.at[1, first + cut - q : first + q]),
                (OUT.at[k, 1, rest:cut], out_out.at[first : first + q]),
            ):
                pltpu.make_async_copy(src, dst, loc.at[4]).start()

    forward(0)
    over_z(2, 0, 0)
    over_z(2, 1, 0)
    forward(1, 0)
    over_z(2, 0, 1)
    over_z(2, 1, 1)
    forward(3, 1)
    forward(2, 3)
    turn(2)
    far = (2, 1, 3)
    tokens_back(0, far)
    x_first(0)
    y_first()
    tokens_back(1, far)
    x_first(1)
    x_second(0)
    tokens_back(2, far)
    x_first(2)
    x_second(1)
    y_next(0)
    tokens_back(3, far)
    x_first(3)
    y_next(1)
    tokens_back(0, (0,))
    x_second(2)
    z_scatter(0)
    tokens_back(1, (0,))
    z_scatter(1)
    x_second(3)
    y_second()
    tokens_back(2, (0,))
    z_middle(0)
    z_scatter(2)
    tokens_back(3, (0,))
    weights_back(y)
    z_middle(1)
    z_gather(0)
    z_scatter(3)
    z_middle(2)
    z_gather(1)
    z_relay(0)
    x_slices()
    z_middle(3)
    z_gather(2)
    z_relay(1)
    z_gather(3)
    z_relay(2)
    z_done(0)
    z_done(1)
    weights_out()
    z_relay(3)
    z_done(2)
    z_done(3)
    for ref, sem in (
        (W, s_w), (X.at[:, :, :, 0 : tok - tok // 8, :], s_x), (PDs, s_pd), (xopp, s_xo), (xs, s_xs), (yopp, s_yo),
        (ys, s_ys), (R.at[:, 0:3], s_r), (Zt.at[:, 0:7], s_z), (G.at[0, 0:3], s_g), (G.at[0], s_gd),
    ):
        sent(ref, sem)
    got(OUT, loc.at[4])
    got(Zf, loc.at[3])


def widen_kernel(*refs):
    for src, dst in zip(refs[:3], refs[3:]):
        dst[...] = src[...].astype(F32)


def widen(tok, w_in, w_out):
    steps = 4
    specs = [
        pl.BlockSpec((tok.shape[0] // steps, tok.shape[1]), lambda i: (i, 0)),
        pl.BlockSpec((2, w_in.shape[1] // steps, w_in.shape[2]), lambda i: (0, i, 0)),
        pl.BlockSpec((w_out.shape[0] // steps, w_out.shape[1]), lambda i: (i, 0)),
    ]
    return pl.pallas_call(
        widen_kernel,
        grid=(steps,),
        in_specs=specs,
        out_specs=specs,
        out_shape=[jax.ShapeDtypeStruct(a.shape, F32) for a in (tok, w_in, w_out)],
    )(tok, w_in, w_out)


def shards(n_z, tokens, tangent, cotangent, expert_ids, gates, w_in, v_in, w_out, v_out):
    tok = tokens.shape[0]
    ff, lanes = w_in.shape[2:]
    width = tokens.shape[1]
    q = ff // SIDE
    half = tok // 2
    part = width // SIDE
    cut = 3 * q // 2
    dma = pltpu.SemaphoreType.DMA
    vmem = pl.BlockSpec(memory_space=pltpu.VMEM)
    hbm = pl.BlockSpec(memory_space=pltpu.HBM)
    y_tok, y_in, y_out = pl.pallas_call(
        functools.partial(kernel, n_z),
        out_shape=(
            jax.ShapeDtypeStruct((n_z, tok // n_z, width), BF16),
            jax.ShapeDtypeStruct((2, ff, lanes), BF16),
            jax.ShapeDtypeStruct((ff, lanes), BF16),
        ),
        in_specs=[vmem, vmem] + [hbm] * 7,
        out_specs=(hbm, hbm, hbm),
        scratch_shapes=[
            pltpu.VMEM((SIDE * SIDE, 6, q, lanes), BF16),
            pltpu.VMEM((6, ff, lanes), BF16),
            pltpu.VMEM((2, 3, q, lanes), BF16),
            pltpu.VMEM((3, SIDE, 2, tok, width), BF16),
            pltpu.VMEM((2, SIDE, 8, tok), F32),
            pltpu.VMEM((8 * q, 2 * tok), F32),
            pltpu.VMEM((4 * q, SIDE * 2 * tok), BF16),
            pltpu.VMEM((4, 2 * tok, 4 * q), BF16),
            pltpu.VMEM((q, SIDE * 2 * tok), BF16),
            pltpu.VMEM((SIDE, 3 * q, part), F32),
            pltpu.VMEM((4, SIDE, tok, part), F32),
            pltpu.VMEM((4, SIDE, tok, part), BF16),
            pltpu.VMEM((4, SIDE, tok, part), BF16),
            pltpu.VMEM((SIDE, 2, 2, half, part), BF16),
            pltpu.VMEM((SIDE, 2, half, part), BF16),
            pltpu.VMEM((SIDE, 2, 2, half, part), BF16),
            pltpu.VMEM((SIDE, 2, half, part), BF16),
            pltpu.VMEM((2, 2, cut, part), BF16),
            pltpu.VMEM((2, cut, part), BF16),
            pltpu.VMEM((2, 2, cut, part), BF16),
            pltpu.VMEM((2, cut, part), BF16),
            pltpu.VMEM((2, SIDE, cut, lanes), BF16),
            pltpu.VMEM((SIDE, 2, cut, lanes), BF16),
            pltpu.VMEM((SIDE, n_z, tok // n_z, part), F32),
            pltpu.VMEM((SIDE, n_z, tok // n_z, part), BF16),
            pltpu.VMEM((SIDE, 2, tok // n_z, part + part // 2), BF16),
            pltpu.VMEM((SIDE, 2, 2, tok // n_z, part), BF16),
            pltpu.VMEM((SIDE, 2, 2, tok // n_z, part), BF16),
            pltpu.VMEM((SIDE, n_z, tok // n_z, part), BF16),
            dma((5,)),
            dma((11,)),
            dma((2, 2)), dma((2,)), dma((2,)),
            dma((2, 4)), dma((1,)),
            dma((2, 2, 2)), dma((2, 2)), dma((3, 2, 2)),
            dma((2,)), dma((4,)), dma((4, 4)),
            dma((4, 2)), dma((4,)),
            dma((2,)), dma((2, 2)), dma((1,)),
            dma((4, 2)), dma((4,)), dma((4,)), dma((4,)),
        ],
        compiler_params=pltpu.CompilerParams(
            collective_id=0, has_side_effects=True, vmem_limit_bytes=62 * 1024 * 1024
        ),
    )(
        expert_ids.T, gates.T, tokens, tangent, cotangent, w_in[0], v_in[0], w_out[0], v_out[0]
    )
    y_tok, y_in, y_out = widen(y_tok.reshape(tok, width), y_in, y_out)
    return y_tok, y_in[None], y_out[None]


def solution(mesh):
    rows = P(("expert", "dp"), None)
    w_spec = P(("tensor", "expert"), None, None, "dp")
    o_spec = P(("tensor", "expert"), None, "dp")
    return jax.shard_map(
        functools.partial(shards, mesh.shape["tensor"]),
        mesh=mesh,
        in_specs=(rows,) * 5 + (w_spec, w_spec, o_spec, o_spec),
        out_specs=(rows, w_spec, o_spec),
        check_vma=False,
    )
```

time: 116 us -> 108 us (0.931)
  Pallas kernels: 111 us -> 107 us
  other arithmetic: 3.87 us -> 0 us
    pallas_call x1, Pallas kernels: 111 us -> 104 us  [shards(): pl.pallas_call(functools.partial(kernel, n_z), out_shape=(jax.ShapeDtypeS...]
    convert_element_type x3 -> x0, other arithmetic: 3.87 us -> none  [shards(): return (y_tok.astype(F32), y_in[None].astype(F32), y_out[None].astype(F32))]
    pallas_call x0 -> x1, Pallas kernels: none -> 3.59 us  [widen(): pl.pallas_call(widen_kernel, grid=(steps,), in_specs=specs, out_specs=spe...]
where the time goes in v3:
time: 108 us
  Pallas kernels  107 us (99%)
    pallas_call x1, Pallas kernels, shards(): pl.pallas_call(functools.partial(kernel, n_z), out_shape=(jax.ShapeDtypeS...  104 us
    pallas_call x1, Pallas kernels, widen(): pl.pallas_call(widen_kernel, grid=(steps,), in_specs=specs, out_specs=spe...  3.59 us

profile of v3, /device:TPU:24, one launch (start us, length us, event | category | flops | bytes accessed | tf_op | source)
XLA Modules:
  0.0 107.7 jit_solution(3604253757482514757)
XLA Ops:
  0.6 103.5 %shard_map.112 = (bf16[8,16,2048]{2,1,0:T(8,128)(2,1)}, bf16[2,768,128]{2,1,0:T(8,128)(2,1)}, bf16[768,128]{1,0:T(8,128)(2,1)}) custom-call(s32[8,128]{1,0:T(8,128)} %bitcast.14, f32[8,128]{1,0:T(8,128)} %bitcast.15, bf16[128,2048]{1,0:T(8,128)(2,1)} %tok_ref.1, bf16[128,2048]{1,0:T(8,128)(2,1)} %tan_ref.1, bf16[128,2048]{1,0:T(8,128)(2,1)} %cot_ref.1, ...), custom_call_target="tpu_custom_call" | custom-call | tf_op jit(solution)/shard_map/pallas_call | solution.py:510
  104.2 3.6 %shard_map.113 = (f32[128,2048]{1,0:T(8,128)}, f32[2,768,128]{2,1,0:T(8,128)}, f32[768,128]{1,0:T(8,128)}) custom-call(bf16[128,2048]{1,0:T(8,128)(2,1)} %bitcast.9, bf16[2,768,128]{2,1,0:T(8,128)(2,1)} %get-tuple-element.10.refs_1_, bf16[768,128]{1,0:T(8,128)(2,1)} %get-tuple-element.11.refs_2_), custom_call_target="tpu_custom_call" | custom-call | tf_op jit(solution)/shard_map/pallas_call | solution.py:490

commit v4 on v3

v4 whole, which is shorter than its diff:
```python
import functools

import jax
import jax.numpy as jnp
from jax import lax
from jax.experimental import pallas as pl
from jax.experimental.pallas import tpu as pltpu
from jax.sharding import PartitionSpec as P

MESH = pl.DeviceIdType.MESH
F32 = jnp.float32
BF16 = jnp.bfloat16
SIDE = 4
NT = (((1,), (1,)), ((), ()))
NN = (((1,), (0,)), ((), ()))


def mm(a, b, dims=NN):
    return lax.dot_general(a, b, dims, preferred_element_type=F32)


def kernel(
    n_z, ids_ref, gates_ref, tok_ref, tan_ref, cot_ref, wi_ref, vi_ref, wo_ref, vo_ref,
    out_tok, out_in, out_out,
    W, Wsrc, stage, X, G, C, S, ST, H, acc, Pown, PDs, PDr, xs, xopp, xr, xropp, ys, yopp, yr, yropp, R, OUT, Zt, Zs, Z3, Zm, Zr, Zf,
    loc, snd, wa_r, st_r, sf_r, wy_r, wrest, xh_r, xf_r, zx_r, g_r, dd_r, pd_r, xo_r, xp_r, yo_r, yp_r, ra_r,
    z1_r, z4_r, z2_r, zd_r,
):
    t = lax.axis_index("tensor")
    e = lax.axis_index("expert")
    p = lax.axis_index("dp")
    y, x = p // SIDE, p % SIDE
    color = lax.rem(t, 2)
    tok = tok_ref.shape[0]
    half = tok // 2
    quarter = tok // 4
    lanes = wi_ref.shape[-1]
    q = W.shape[2]
    width = tok_ref.shape[1]
    part = width // SIDE

    def at_x(d):
        return lax.rem(x + d, SIDE)

    def at_y(d):
        return lax.rem(y + d, SIDE)

    def dev_x(d):
        return (t, e, y * SIDE + at_x(d))

    def dev_y(d):
        return (t, e, at_y(d) * SIDE + x)

    def dev_z(d):
        return (lax.rem(t + d, n_z), e, p)

    partner = (t, 1 - e, p)
    s_w, s_x, s_pd, s_xo, s_xs, s_yo, s_ys, s_r, s_z, s_g, s_gd = (snd.at[i] for i in range(11))

    def send(src, dst, ssem, rsem, dev):
        pltpu.make_async_remote_copy(
            src_ref=src, dst_ref=dst, send_sem=ssem, recv_sem=rsem, device_id=dev, device_id_type=MESH
        ).start()

    def got(ref, rsem):
        pltpu.make_async_remote_copy(
            src_ref=ref, dst_ref=ref, send_sem=s_w, recv_sem=rsem, device_id=partner, device_id_type=MESH
        ).wait_recv()

    def sent(ref, ssem):
        pltpu.make_async_remote_copy(
            src_ref=ref, dst_ref=ref, send_sem=ssem, recv_sem=ssem, device_id=partner, device_id_type=MESH
        ).wait_send()

    barrier = pltpu.get_barrier_semaphore()
    peers = [partner] + [dev_x(d) for d in (1, 2, 3)] + [dev_y(d) for d in (1, 3)] + [dev_z(d) for d in (1, 2, n_z - 2, n_z - 1)]
    for peer in peers:
        pl.semaphore_signal(barrier, inc=1, device_id=peer, device_id_type=MESH)

    def rows(k):
        return pl.ds(pl.multiple_of(k * q, q), q)

    for src, dst, i in (
        (wi_ref, Wsrc.at[0:2], 0),
        (wo_ref, Wsrc.at[2], 0),
        (vi_ref, Wsrc.at[3:5], 0),
        (vo_ref, Wsrc.at[5], 0),
        (wi_ref.at[:, rows(x), :], W.at[p, 0:2], 1),
        (wo_ref.at[rows(x), :], W.at[p, 2], 1),
        (vi_ref.at[:, rows(x), :], W.at[p, 3:5], 1),
        (vo_ref.at[rows(x), :], W.at[p, 5], 1),
        (tok_ref, X.at[0, x, e], 2),
        (tan_ref, X.at[1, x, e], 2),
        (cot_ref, X.at[2, x, e], 2),
    ):
        pltpu.make_async_copy(src, dst, loc.at[i]).start()
    ids, gates = ids_ref[...], gates_ref[...]
    for r in range(2):
        G[e, x, pl.ds(r, 1), :] = jnp.sum(jnp.where(ids == 2 * t + r, gates, 0.0), axis=0, keepdims=True)
    pl.semaphore_wait(barrier, len(peers))

    got(Wsrc, loc.at[0])

    def quarter_of(h, k):
        return Wsrc.at[3 * h : 3 * h + 3, rows(k), :]

    def unit(yy, d, h):
        return W.at[yy * SIDE + at_x(SIDE - d), 3 * h : 3 * h + 3]

    def quarter_to(h):
        for k, d in enumerate((1, 3)):
            send(quarter_of(h, at_x(d)), unit(y, 0, h), s_w, wa_r.at[k, h], dev_x(d))

    quarter_to(0)
    for h in range(2):
        send(quarter_of(h, at_x(2)), stage.at[h], s_w, st_r.at[h], dev_x(1 + 2 * h))
    quarter_to(1)
    for d in (1, 3, 2):
        send(G.at[e, x], G.at[e, x], s_g, g_r.at[0], dev_x(d))
    got(W.at[p], loc.at[1])

    order = (0, 1, 3, 2)

    def spread(d, h):
        k = order.index(d)
        for i in range(2):
            sem = wy_r.at[i, k] if i == h else wrest.at[1]
            send(unit(y, d, h), unit(y, d, h), s_w, sem, dev_y(1 + 2 * i))

    def onward(d):
        k = order.index(d)
        for h in range(2):
            at = unit(at_y(3 - 2 * h), d, h)
            got(at, wy_r.at[h, k])
            send(at, at, s_w, wrest.at[0], dev_y(1 + 2 * h))

    def got_quarter(h):
        for k, d in enumerate((1, 3)):
            got(unit(y, d, h), wa_r.at[k, h])
            spread(d, h)

    spread(0, 0)
    spread(0, 1)
    got(X.at[:, x, e], loc.at[2])

    def piece(a, own, h, i):
        eighth = quarter // 2
        first = (color if own else 1 - color) * half + h * quarter + i * eighth
        return X.at[:, a, e, pl.ds(pl.multiple_of(first, eighth), eighth), :]

    def over_links(k, h, i):
        at = piece(x, True, h, i)
        send(at, at, s_x, xh_r.at[k, h, i], dev_x(1 + 2 * k))

    over_links(0, 0, 0)
    over_links(1, 1, 0)
    send(X.at[:, x, e], X.at[:, x, e], s_x, dd_r.at[0], partner)
    got_quarter(0)
    for h in range(2):
        got(stage.at[h], st_r.at[h])
        send(stage.at[h], unit(y, 1 + 2 * h, h), s_w, sf_r.at[h], dev_x(1 + 2 * h))
    for k, h, i in ((0, 0, 1), (1, 1, 1), (0, 1, 0), (1, 0, 0), (0, 1, 1), (1, 0, 1)):
        over_links(k, h, i)

    def over_x(rel, h, i):
        at = piece(at_x(SIDE - rel), True, h, i)
        if rel == 2:
            got(at, xf_r.at[h, i])
        else:
            k = rel // 2
            got(at, xh_r.at[k, h, i])
            if h == k:
                send(at, at, s_x, xf_r.at[h, i], dev_x(1 + 2 * k))
        send(at, at, s_x, zx_r.at[rel - 1, h, i], dev_z(1 if h == 0 else n_z - 1))
        send(at, at, s_x, dd_r.at[rel], partner)

    def over_z(rel, h, i):
        at = piece(at_x(SIDE - rel), False, h, i)
        got(at, zx_r.at[rel - 1, h, i])
        send(at, at, s_x, dd_r.at[rel], partner)

    n_acc = acc.shape[1]
    cut = n_acc // 2
    step = 32

    def tokens_of(a):
        return pl.ds(pl.multiple_of(a * 2 * tok, 2 * tok), 2 * tok)

    def weights(lo, hi, slabs=range(SIDE * SIDE)):
        return jnp.concatenate([W[k, lo:hi].reshape((hi - lo) * q, lanes) for k in slabs], axis=1)

    def turn(rel):
        ST[rel] = S[:, tokens_of(at_x(SIDE - rel))].T

    def products(rel, quarters, add):
        a = at_x(SIDE - rel)
        if not add:
            got(X.at[:, a, 1 - e], dd_r.at[rel])
        slabs = [at_y(d) * SIDE + k for d in quarters for k in range(SIDE)]
        for first, lo, hi, i in ((0, 0, 2, 0), (2, 3, 5, 0), (4, 0, 2, 1), (6, 2, 3, 2), (7, 5, 6, 2)):
            cols = [pl.ds(pl.multiple_of(at_y(d) * part, part), part) for d in quarters]
            right = jnp.concatenate([X[i, a, :, :, c].reshape(2 * tok, part) for c in cols], axis=1)
            value = mm(weights(lo, hi, slabs), right, NT)
            at = slice(first * q, (first + hi - lo) * q)
            C[rel, at, :] = C[rel, at, :] + value if add else value

    def forward(rel, before=None):
        a = at_x(SIDE - rel)
        if before is not None:
            turn(before)
        products(rel, (2,) if rel == 0 else (0, 1, 3, 2), rel == 0)
        gate = jnp.concatenate([G[0, a, pl.ds(e, 1), :], G[1, a, pl.ds(e, 1), :]], axis=1)
        cols = tokens_of(a)

        def rows_of(i, carry):
            at = pl.multiple_of(i * step, step)

            def c(k):
                return C[rel, pl.ds(k * q + at, step), :]

            pre, up = c(0), c(1)
            pre_dot, up_dot = c(4) + c(2), c(5) + c(3)
            g, g_dot = c(6) * gate, c(7) * gate
            sigma = jax.nn.sigmoid(pre)
            rest = 1.0 - sigma
            s0 = pre * sigma
            s1 = sigma * (1.0 + pre * rest)
            s2 = sigma * rest * (2.0 + pre * (1.0 - 2.0 * sigma))
            S[pl.ds(at, step), cols] = (
                g_dot * up * s1 + g * up_dot * s1 + g * up * s2 * pre_dot
            ).astype(BF16)
            S[pl.ds(q + at, step), cols] = (g_dot * s0 + g * s1 * pre_dot).astype(BF16)
            S[pl.ds(2 * q + at, step), cols] = (g * up * s1).astype(BF16)
            S[pl.ds(3 * q + at, step), cols] = (g * s0).astype(BF16)
            H[pl.ds(at, step), cols] = ((s1 * pre_dot * up + s0 * up_dot) * gate).astype(BF16)
            return carry

        lax.fori_loop(0, q // step, rows_of, 0)

    def tokens_back(n, rels):
        slabs = range(SIDE * n, SIDE * n + SIDE)
        for rel in rels:
            left = jnp.concatenate(
                [ST[rel, pl.ds(pl.multiple_of(k * tok, tok), tok), :] for k in (e, 1 - e)], axis=0
            )
            value = mm(left[:, 0 : 2 * q], weights(0, 2, slabs)) + mm(left[:, 2 * q : 4 * q], weights(3, 5, slabs))
            Pown[rel, n] = value[0:tok]
            PDs[rel, n] = value[tok : 2 * tok].astype(BF16)
            send(PDs.at[rel, n], PDr.at[rel, n], s_pd, pd_r.at[rel, n], partner)

    def weights_back(n):
        cols = pl.ds(pl.multiple_of(n * part, part), part)

        def every(i):
            return X[i, :, :, :, cols].reshape(SIDE * 2 * tok, part)

        acc[n, 0 : 2 * q, :] = mm(S[2 * q : 4 * q, :], every(1)) + mm(S[0 : 2 * q, :], every(0))
        acc[n, 2 * q : 3 * q, :] = mm(H[...], every(2))

    def summed(rel, n, h):
        at = pl.ds(h * half, half)
        return Pown[rel, n, at, :] + PDr[rel, n, at, :].astype(F32)

    def acc_half(k, h):
        return acc[k, h * cut : (h + 1) * cut, :]

    def x_far(n):
        got(PDr.at[2, n], pd_r.at[2, n])
        for h in range(2):
            xopp[n, h] = summed(2, n, h).astype(BF16)
            send(xopp.at[n, h], xropp.at[n, h], s_xo, xo_r.at[n, h], dev_x(1 + 2 * h))

    def x_near(n):
        for rel, k, h in ((1, 1, 0), (3, 0, 1)):
            got(PDr.at[rel, n], pd_r.at[rel, n])
            xs[n, k, h] = summed(rel, n, h).astype(BF16)
            send(xs.at[n, k, h], xr.at[n, k, h], s_xs, xp_r.at[n], dev_x(1 + 2 * k))

    def x_second(n):
        for k in range(2):
            got(xropp.at[n, k], xo_r.at[n, k])
            xs[n, k, k] = (summed(3 - 2 * k, n, k) + xropp[n, k].astype(F32)).astype(BF16)
            send(xs.at[n, k, k], xr.at[n, k, k], s_xs, xp_r.at[n], dev_x(1 + 2 * k))

    piece_z = tok // n_z

    def at_z(d):
        return lax.rem(t + d + n_z, n_z)

    mid = part // 2

    def lane_half(h):
        return slice(h * mid, (h + 1) * mid)

    def z_scatter(n):
        got(PDr.at[0, n], pd_r.at[0, n])
        got(xr.at[n], xp_r.at[n])
        for h in range(2):
            total = summed(0, n, h) + xr[n, 0, h].astype(F32) + xr[n, 1, h].astype(F32)
            total = total.reshape(n_z // 2, piece_z, part)
            at = pl.ds(h * (n_z // 2), n_z // 2)
            Zt[n, at] = total
            Zs[n, at] = total.astype(BF16)
        for k in range(2):
            far = at_z(3 - 6 * k)
            send(Zs.at[n, far], Z3.at[n, k, :, 0:part], s_z, z1_r.at[n, k], dev_z(2 + (n_z - 4) * k))
            src = Zs.at[n, at_z(4), :, lane_half(k)]
            send(src, Z3.at[n, k, :, part:], s_z, z1_r.at[n, k], dev_z(2 + (n_z - 4) * k))

    def z_middle(n):
        for k in range(2):
            sign = 1 - 2 * k
            got(Z3.at[n, k], z1_r.at[n, k])
            Zm[n, 0, k] = (Zt[n, at_z(sign)] + Z3[n, k, :, 0:part].astype(F32)).astype(BF16)
            send(Zm.at[n, 0, k], Zr.at[n, 0, k], s_z, z4_r.at[n], dev_z((sign + n_z) % n_z))
            here, there = lane_half(k), lane_half(1 - k)
            next_but_one = at_z(2 * sign)
            Zm[n, 1, k, :, here] = (Zt[n, next_but_one, :, here] + Z3[n, k, :, part:].astype(F32)).astype(BF16)
            Zm[n, 1, k, :, there] = Zt[n, next_but_one, :, there].astype(BF16)
            send(Zm.at[n, 1, k], Zr.at[n, 1, k], s_z, z4_r.at[n], dev_z((2 * sign + n_z) % n_z))

    def z_gather(n):
        done = Zt[n, t]
        got(Zr.at[n], z4_r.at[n])
        for i in range(2):
            for k in range(2):
                done += Zr[n, i, k].astype(F32)
        Zf[n, t] = done.astype(BF16)
        for i in (1, 0):
            for k in range(2):
                d = (i + 1) * (1 - 2 * k)
                sem = (zd_r if i == 0 else z2_r).at[n]
                send(Zf.at[n, t], Zf.at[n, t], s_z, sem, dev_z((d + n_z) % n_z))

    def z_relay(n):
        got(Zf.at[n, 0:2], z2_r.at[n])
        for k in range(2):
            sign = 1 - 2 * k
            src = at_z(-2 * sign)
            send(Zf.at[n, src], Zf.at[n, src], s_z, zd_r.at[n], dev_z((sign + n_z) % n_z))
            at = Zf.at[n, src, :, lane_half(k)]
            send(at, at, s_z, zd_r.at[n], dev_z((2 * sign + n_z) % n_z))

    def z_done(n):
        got(Zf.at[n, 0:5], zd_r.at[n])
        pltpu.make_async_copy(Zf.at[n], out_tok.at[:, :, n * part : (n + 1) * part], loc.at[3]).start()

    def y_first():
        weights_back(at_y(2))
        for h in range(2):
            yopp[h] = acc_half(at_y(2), h).astype(BF16)
            send(yopp.at[h], yropp.at[h], s_yo, yo_r.at[h], dev_y(1 + 2 * h))

    def y_next(k):
        h = 1 - k
        weights_back(at_y(1 + 2 * k))
        ys[k, h] = acc_half(at_y(1 + 2 * k), h).astype(BF16)
        send(ys.at[k, h], yr.at[k, h], s_ys, yp_r.at[k, h], dev_y(1 + 2 * k))

    def y_second():
        for k in range(2):
            got(yropp.at[k], yo_r.at[k])
            ys[k, k] = (acc_half(at_y(1 + 2 * k), k) + yropp[k].astype(F32)).astype(BF16)
            send(ys.at[k, k], yr.at[k, k], s_ys, yp_r.at[k, k], dev_y(1 + 2 * k))

    def x_slices():
        for h in range(2):
            for k in range(2):
                got(yr.at[k, h], yp_r.at[k, h])
            value = acc_half(y, h) + yr[0, h].astype(F32) + yr[1, h].astype(F32)
            value = value.astype(BF16)
            for k in range(SIDE):
                R[h, k] = value[:, k * lanes : (k + 1) * lanes]
            OUT[x, h] = R[h, x]
            for d in (1, 3, 2):
                send(R.at[h, at_x(d)], OUT.at[x, h], s_r, ra_r.at[0], dev_x(d))

    def weights_out():
        got(OUT.at[0:3], ra_r.at[0])
        for k in range(SIDE):
            first, rest = k * q, n_acc - cut - q
            for src, dst in (
                (OUT.at[k, 0, 0:q], out_in.at[0, first : first + q]),
                (OUT.at[k, 0, q:cut], out_in.at[1, first : first + cut - q]),
                (OUT.at[k, 1, 0:rest], out_in.at[1, first + cut - q : first + q]),
                (OUT.at[k, 1, rest:cut], out_out.at[first : first + q]),
            ):
                pltpu.make_async_copy(src, dst, loc.at[4]).start()

    got_quarter(1)
    for h in range(2):
        got(unit(y, 2, h), sf_r.at[h])
        spread(2, h)
    onward(0)
    onward(1)
    over_x(1, 0, 0)
    over_x(3, 1, 0)
    got(G.at[e, 0:3], g_r.at[0])
    send(G.at[e], G.at[e], s_gd, g_r.at[1], partner)
    onward(3)
    over_x(1, 0, 1)
    over_x(3, 1, 1)
    over_z(1, 0, 0)
    over_z(3, 1, 0)
    onward(2)
    over_x(1, 1, 0)
    over_x(3, 0, 0)
    over_z(1, 0, 1)
    over_z(3, 1, 1)
    got(W.at[0:4], wrest.at[1])
    products(0, (0, 1, 3), False)
    over_x(1, 1, 1)
    over_x(3, 0, 1)
    over_z(3, 0, 0)
    over_z(1, 1, 0)
    over_x(2, 0, 0)
    over_x(2, 1, 0)
    over_z(3, 0, 1)
    over_z(1, 1, 1)
    over_x(2, 0, 1)
    over_x(2, 1, 1)
    got(W.at[0:4], wrest.at[0])
    got(G.at[1 - e], g_r.at[1])
    forward(1)
    over_z(2, 0, 0)
    over_z(2, 1, 0)
    forward(3, 1)
    over_z(2, 0, 1)
    over_z(2, 1, 1)
    forward(0, 3)
    near, far = (1, 3), (2, 1, 3)
    tokens_back(0, near)
    tokens_back(1, near)
    x_near(0)
    forward(2, 0)
    turn(2)
    x_near(1)
    tokens_back(0, (2,))
    tokens_back(1, (2,))
    x_far(0)
    y_first()
    x_far(1)
    tokens_back(0, (0,))
    tokens_back(1, (0,))
    x_second(0)
    tokens_back(2, far)
    x_second(1)
    y_next(0)
    x_far(2)
    x_near(2)
    y_next(1)
    z_scatter(0)
    tokens_back(3, far)
    x_second(2)
    z_scatter(1)
    x_far(3)
    x_near(3)
    z_middle(0)
    y_second()
    tokens_back(2, (0,))
    tokens_back(3, (0,))
    z_middle(1)
    x_second(3)
    z_scatter(2)
    z_gather(0)
    weights_back(y)
    z_gather(1)
    z_middle(2)
    z_scatter(3)
    z_relay(0)
    z_relay(1)
    z_gather(2)
    z_middle(3)
    x_slices()
    z_relay(2)
    z_gather(3)
    z_done(0)
    z_done(1)
    z_relay(3)
    weights_out()
    z_done(2)
    z_done(3)
    for ref, sem in (
        (W, s_w), (X.at[:, :, :, 0 : tok - tok // 8, :], s_x), (PDs, s_pd), (xopp, s_xo), (xs, s_xs), (yopp, s_yo),
        (ys, s_ys), (R.at[:, 0:3], s_r), (Zt.at[:, 0:7], s_z), (G.at[0, 0:3], s_g), (G.at[0], s_gd),
    ):
        sent(ref, sem)
    got(OUT, loc.at[4])
    got(Zf, loc.at[3])


def widen_kernel(*refs):
    for src, dst in zip(refs[:3], refs[3:]):
        dst[...] = src[...].astype(F32)


def widen(tok, w_in, w_out):
    steps = 4
    specs = [
        pl.BlockSpec((tok.shape[0] // steps, tok.shape[1]), lambda i: (i, 0)),
        pl.BlockSpec((2, w_in.shape[1] // steps, w_in.shape[2]), lambda i: (0, i, 0)),
        pl.BlockSpec((w_out.shape[0] // steps, w_out.shape[1]), lambda i: (i, 0)),
    ]
    return pl.pallas_call(
        widen_kernel,
        grid=(steps,),
        in_specs=specs,
        out_specs=specs,
        out_shape=[jax.ShapeDtypeStruct(a.shape, F32) for a in (tok, w_in, w_out)],
    )(tok, w_in, w_out)


def shards(n_z, tokens, tangent, cotangent, expert_ids, gates, w_in, v_in, w_out, v_out):
    tok = tokens.shape[0]
    ff, lanes = w_in.shape[2:]
    width = tokens.shape[1]
    q = ff // SIDE
    half = tok // 2
    part = width // SIDE
    cut = 3 * q // 2
    dma = pltpu.SemaphoreType.DMA
    vmem = pl.BlockSpec(memory_space=pltpu.VMEM)
    hbm = pl.BlockSpec(memory_space=pltpu.HBM)
    y_tok, y_in, y_out = pl.pallas_call(
        functools.partial(kernel, n_z),
        out_shape=(
            jax.ShapeDtypeStruct((n_z, tok // n_z, width), BF16),
            jax.ShapeDtypeStruct((2, ff, lanes), BF16),
            jax.ShapeDtypeStruct((ff, lanes), BF16),
        ),
        in_specs=[vmem, vmem] + [hbm] * 7,
        out_specs=(hbm, hbm, hbm),
        scratch_shapes=[
            pltpu.VMEM((SIDE * SIDE, 6, q, lanes), BF16),
            pltpu.VMEM((6, ff, lanes), BF16),
            pltpu.VMEM((2, 3, q, lanes), BF16),
            pltpu.VMEM((3, SIDE, 2, tok, width), BF16),
            pltpu.VMEM((2, SIDE, 8, tok), F32),
            pltpu.VMEM((4, 8 * q, 2 * tok), F32),
            pltpu.VMEM((4 * q, SIDE * 2 * tok), BF16),
            pltpu.VMEM((4, 2 * tok, 4 * q), BF16),
            pltpu.VMEM((q, SIDE * 2 * tok), BF16),
            pltpu.VMEM((SIDE, 3 * q, part), F32),
            pltpu.VMEM((4, SIDE, tok, part), F32),
            pltpu.VMEM((4, SIDE, tok, part), BF16),
            pltpu.VMEM((4, SIDE, tok, part), BF16),
            pltpu.VMEM((SIDE, 2, 2, half, part), BF16),
            pltpu.VMEM((SIDE, 2, half, part), BF16),
            pltpu.VMEM((SIDE, 2, 2, half, part), BF16),
            pltpu.VMEM((SIDE, 2, half, part), BF16),
            pltpu.VMEM((2, 2, cut, part), BF16),
            pltpu.VMEM((2, cut, part), BF16),
            pltpu.VMEM((2, 2, cut, part), BF16),
            pltpu.VMEM((2, cut, part), BF16),
            pltpu.VMEM((2, SIDE, cut, lanes), BF16),
            pltpu.VMEM((SIDE, 2, cut, lanes), BF16),
            pltpu.VMEM((SIDE, n_z, tok // n_z, part), F32),
            pltpu.VMEM((SIDE, n_z, tok // n_z, part), BF16),
            pltpu.VMEM((SIDE, 2, tok // n_z, part + part // 2), BF16),
            pltpu.VMEM((SIDE, 2, 2, tok // n_z, part), BF16),
            pltpu.VMEM((SIDE, 2, 2, tok // n_z, part), BF16),
            pltpu.VMEM((SIDE, n_z, tok // n_z, part), BF16),
            dma((5,)),
            dma((11,)),
            dma((2, 2)), dma((2,)), dma((2,)),
            dma((2, 4)), dma((2,)),
            dma((2, 2, 2)), dma((2, 2)), dma((3, 2, 2)),
            dma((2,)), dma((4,)), dma((4, 4)),
            dma((4, 2)), dma((4,)),
            dma((2,)), dma((2, 2)), dma((1,)),
            dma((4, 2)), dma((4,)), dma((4,)), dma((4,)),
        ],
        compiler_params=pltpu.CompilerParams(
            collective_id=0, has_side_effects=True, vmem_limit_bytes=62 * 1024 * 1024
        ),
    )(
        expert_ids.T, gates.T, tokens, tangent, cotangent, w_in[0], v_in[0], w_out[0], v_out[0]
    )
    y_tok, y_in, y_out = widen(y_tok.reshape(tok, width), y_in, y_out)
    return y_tok, y_in[None], y_out[None]


def solution(mesh):
    rows = P(("expert", "dp"), None)
    w_spec = P(("tensor", "expert"), None, None, "dp")
    o_spec = P(("tensor", "expert"), None, "dp")
    return jax.shard_map(
        functools.partial(shards, mesh.shape["tensor"]),
        mesh=mesh,
        in_specs=(rows,) * 5 + (w_spec, w_spec, o_spec, o_spec),
        out_specs=(rows, w_spec, o_spec),
        check_vma=False,
    )
```

time: 108 us -> 108 us (level)
  no operation moved by 1% of the time
where the time goes in v4:
time: 108 us; the launch traced here: 107 us
  Pallas kernels  107 us (99%)
    pallas_call x1, Pallas kernels, shards(): pl.pallas_call(functools.partial(kernel, n_z), out_shape=(jax.ShapeDtypeS...  103 us
    pallas_call x1, Pallas kernels, widen(): pl.pallas_call(widen_kernel, grid=(steps,), in_specs=specs, out_specs=spe...  3.59 us

profile of v4, /device:TPU:24, one launch (start us, length us, event | category | flops | bytes accessed | tf_op | source)
XLA Modules:
  0.0 107.4 jit_solution(3718380353762695206)
XLA Ops:
  0.6 103.1 %shard_map.112 = (bf16[8,16,2048]{2,1,0:T(8,128)(2,1)}, bf16[2,768,128]{2,1,0:T(8,128)(2,1)}, bf16[768,128]{1,0:T(8,128)(2,1)}) custom-call(s32[8,128]{1,0:T(8,128)} %bitcast.14, f32[8,128]{1,0:T(8,128)} %bitcast.15, bf16[128,2048]{1,0:T(8,128)(2,1)} %tok_ref.1, bf16[128,2048]{1,0:T(8,128)(2,1)} %tan_ref.1, bf16[128,2048]{1,0:T(8,128)(2,1)} %cot_ref.1, ...), custom_call_target="tpu_custom_call" | custom-call | tf_op jit(solution)/shard_map/pallas_call | solution.py:524
  103.8 3.6 %shard_map.113 = (f32[128,2048]{1,0:T(8,128)}, f32[2,768,128]{2,1,0:T(8,128)}, f32[768,128]{1,0:T(8,128)}) custom-call(bf16[128,2048]{1,0:T(8,128)(2,1)} %bitcast.9, bf16[2,768,128]{2,1,0:T(8,128)(2,1)} %get-tuple-element.10.refs_1_, bf16[768,128]{1,0:T(8,128)(2,1)} %get-tuple-element.11.refs_2_), custom_call_target="tpu_custom_call" | custom-call | tf_op jit(solution)/shard_map/pallas_call | solution.py:504

commit v5 on v4

--- a/solution.py
+++ b/solution.py
@@ -440,43 +440,43 @@
     x_far(0)
     y_first()
     x_far(1)
-    tokens_back(0, (0,))
-    tokens_back(1, (0,))
+    tokens_back(2, far)
     x_second(0)
-    tokens_back(2, far)
+    tokens_back(3, far)
+    x_far(2)
+    x_near(2)
     x_second(1)
     y_next(0)
-    x_far(2)
-    x_near(2)
-    y_next(1)
-    z_scatter(0)
-    tokens_back(3, far)
-    x_second(2)
-    z_scatter(1)
     x_far(3)
     x_near(3)
+    y_next(1)
+    tokens_back(0, (0,))
+    x_second(2)
+    z_scatter(0)
+    tokens_back(1, (0,))
+    tokens_back(2, (0,))
+    z_scatter(1)
+    tokens_back(3, (0,))
+    y_second()
     z_middle(0)
-    y_second()
-    tokens_back(2, (0,))
-    tokens_back(3, (0,))
-    z_middle(1)
+    weights_back(y)
     x_second(3)
     z_scatter(2)
+    z_middle(1)
     z_gather(0)
-    weights_back(y)
+    z_scatter(3)
+    z_middle(2)
     z_gather(1)
-    z_middle(2)
-    z_scatter(3)
     z_relay(0)
+    z_middle(3)
+    z_gather(2)
+    x_slices()
     z_relay(1)
-    z_gather(2)
-    z_middle(3)
-    x_slices()
+    z_gather(3)
     z_relay(2)
-    z_gather(3)
     z_done(0)
+    z_relay(3)
     z_done(1)
-    z_relay(3)
     weights_out()
     z_done(2)
     z_done(3)

time: 108 us -> 105 us (0.972)
  Pallas kernels: 107 us -> 104 us
    pallas_call x1, Pallas kernels: 103 us -> 100 us  [shards(): pl.pallas_call(functools.partial(kernel, n_z), out_shape=(jax.ShapeDtypeS...]
where the time goes in v5:
time: 105 us
  Pallas kernels  104 us (99%)
    pallas_call x1, Pallas kernels, shards(): pl.pallas_call(functools.partial(kernel, n_z), out_shape=(jax.ShapeDtypeS...  100 us
    pallas_call x1, Pallas kernels, widen(): pl.pallas_call(widen_kernel, grid=(steps,), in_specs=specs, out_specs=spe...  3.59 us

profile of v5, /device:TPU:24, one launch (start us, length us, event | category | flops | bytes accessed | tf_op | source)
XLA Modules:
  0.0 104.5 jit_solution(5624502514346040644)
XLA Ops:
  0.6 100.3 %shard_map.112 = (bf16[8,16,2048]{2,1,0:T(8,128)(2,1)}, bf16[2,768,128]{2,1,0:T(8,128)(2,1)}, bf16[768,128]{1,0:T(8,128)(2,1)}) custom-call(s32[8,128]{1,0:T(8,128)} %bitcast.14, f32[8,128]{1,0:T(8,128)} %bitcast.15, bf16[128,2048]{1,0:T(8,128)(2,1)} %tok_ref.1, bf16[128,2048]{1,0:T(8,128)(2,1)} %tan_ref.1, bf16[128,2048]{1,0:T(8,128)(2,1)} %cot_ref.1, ...), custom_call_target="tpu_custom_call" | custom-call | tf_op jit(solution)/shard_map/pallas_call | solution.py:524
  100.9 3.6 %shard_map.113 = (f32[128,2048]{1,0:T(8,128)}, f32[2,768,128]{2,1,0:T(8,128)}, f32[768,128]{1,0:T(8,128)}) custom-call(bf16[128,2048]{1,0:T(8,128)(2,1)} %bitcast.9, bf16[2,768,128]{2,1,0:T(8,128)(2,1)} %get-tuple-element.10.refs_1_, bf16[768,128]{1,0:T(8,128)(2,1)} %get-tuple-element.11.refs_2_), custom_call_target="tpu_custom_call" | custom-call | tf_op jit(solution)/shard_map/pallas_call | solution.py:504

commit v6 on v5

--- a/solution.py
+++ b/solution.py
@@ -495,7 +495,7 @@
 
 
 def widen(tok, w_in, w_out):
-    steps = 4
+    steps = 1
     specs = [
         pl.BlockSpec((tok.shape[0] // steps, tok.shape[1]), lambda i: (i, 0)),
         pl.BlockSpec((2, w_in.shape[1] // steps, w_in.shape[2]), lambda i: (0, i, 0)),

time: 105 us -> 104 us (level)
  no operation moved by 1% of the time
where the time goes in v6:
time: 104 us
  Pallas kernels  103 us (99%)
    pallas_call x1, Pallas kernels, shards(): pl.pallas_call(functools.partial(kernel, n_z), out_shape=(jax.ShapeDtypeS...  100 us
    pallas_call x1, Pallas kernels, widen(): pl.pallas_call(widen_kernel, grid=(steps,), in_specs=specs, out_specs=spe...  2.61 us

profile of v6, /device:TPU:24, one launch (start us, length us, event | category | flops | bytes accessed | tf_op | source)
XLA Modules:
  0.0 103.5 jit_solution(6458326238267034835)
XLA Ops:
  0.6 100.3 %shard_map.112 = (bf16[8,16,2048]{2,1,0:T(8,128)(2,1)}, bf16[2,768,128]{2,1,0:T(8,128)(2,1)}, bf16[768,128]{1,0:T(8,128)(2,1)}) custom-call(s32[8,128]{1,0:T(8,128)} %bitcast.14, f32[8,128]{1,0:T(8,128)} %bitcast.15, bf16[128,2048]{1,0:T(8,128)(2,1)} %tok_ref.1, bf16[128,2048]{1,0:T(8,128)(2,1)} %tan_ref.1, bf16[128,2048]{1,0:T(8,128)(2,1)} %cot_ref.1, ...), custom_call_target="tpu_custom_call" | custom-call | tf_op jit(solution)/shard_map/pallas_call | solution.py:524
  100.9 2.6 %shard_map.113 = (f32[128,2048]{1,0:T(8,128)}, f32[2,768,128]{2,1,0:T(8,128)}, f32[768,128]{1,0:T(8,128)}) custom-call(bf16[128,2048]{1,0:T(8,128)(2,1)} %bitcast.9, bf16[2,768,128]{2,1,0:T(8,128)(2,1)} %get-tuple-element.10.refs_1_, bf16[768,128]{1,0:T(8,128)(2,1)} %get-tuple-element.11.refs_2_), custom_call_target="tpu_custom_call" | custom-call | tf_op jit(solution)/shard_map/pallas_call | solution.py:504
